TPU v7x, 32 devices: a whole 2x2x4 slice. The times are simulated.
32 devices in a mesh: seq: 16 (over z, y, x), head: 2 (over core).
Axes of the slice: x: 2, y: 2, z: 4, core: 2. Of those that a mesh axis runs over, the one named last changes fastest.
Arguments:
- queries: bfloat16 [32768, 1024], P('seq', 'head'), may hold values from -10 to 10
- key_vectors: bfloat16 [32768, 1024], P('seq', 'head'), may hold values from -10 to 10
- value_vectors: bfloat16 [32768, 1024], P('seq', 'head'), may hold values from -6 to 6
- grad_output: bfloat16 [32768, 1024], P('seq', 'head'), may hold values from -6 to 6
Outputs:
- attended: bfloat16 [32768, 1024], P('seq', 'head')
- grad_queries: bfloat16 [32768, 1024], P('seq', 'head')
- grad_keys: bfloat16 [32768, 1024], P('seq', 'head')
- grad_values: bfloat16 [32768, 1024], P('seq', 'head')
All inputs are finite; a program needn't handle non-finite values.
Results may differ from a plain program's by a relative error of at most 0.019.
Values may be sent and summed in bfloat16 or wider, within the bound.
A program may use at most 128 MiB of HBM per device.

v0:
```python
import functools
import math

import jax
import jax.numpy as jnp
from jax import lax
from jax.experimental import pallas as pl
from jax.experimental.pallas import tpu as pltpu
from jax.sharding import PartitionSpec as P

ROW_LEN = 512
HEAD_DIM = 128
GROUP = 8
CHUNK = 256
PIECES = 2
MASKED = -1e30
FLOOR = -1e20
LOG2E = 1.0 / math.log(2.0)
SCALE = 1.0 / math.sqrt(HEAD_DIM)
F32 = jnp.float32
BF16 = jnp.bfloat16


def dot_t(left, right):
    return lax.dot_general(left, right, (((1,), (1,)), ((), ())), preferred_element_type=F32)


def dot_f(left, right):
    return lax.dot_general(left, right, (((0,), (0,)), ((), ())), preferred_element_type=F32)


def dot(left, right):
    return jnp.dot(left, right, preferred_element_type=F32)


def row_bias(first, key_chunk, query_chunk):
    if key_chunk < query_chunk:
        return None
    keys = lax.broadcasted_iota(jnp.int32, (CHUNK, CHUNK), 0)
    queries = lax.broadcasted_iota(jnp.int32, (CHUNK, CHUNK), 1)
    return jnp.where(keys <= queries, 0.0, MASKED)


def col_bias(first, key_chunk, query_chunk):
    keys = lax.broadcasted_iota(jnp.int32, (CHUNK, CHUNK), 0)
    queries = lax.broadcasted_iota(jnp.int32, (CHUNK, CHUNK), 1)
    gap = queries - keys
    same = (gap & (GROUP - 1)) == 0
    if key_chunk == query_chunk:
        same = same & (gap > 0)
    return jnp.where(same, 0.0, MASKED)


def chunk(array, index):
    return array[index * CHUNK : (index + 1) * CHUNK]


def scores_of(query, keys, bias, query_chunk):
    out = []
    for j in range(query_chunk + 1):
        s = dot_t(chunk(keys, j), query) * (SCALE * LOG2E)
        b = bias(None, j, query_chunk)
        out.append(s if b is None else s + b)
    return out


def softmax_of(scores, values):
    top = functools.reduce(
        jnp.maximum, [jnp.max(s, axis=0, keepdims=True) for s in scores]
    )
    top = jnp.maximum(top, FLOOR)
    weights = [jnp.exp2(s - top) for s in scores]
    total = sum(jnp.sum(w, axis=0, keepdims=True) for w in weights)
    acc = sum(dot_f(chunk(values, j), w.astype(BF16)) for j, w in enumerate(weights))
    total = jnp.maximum(total, 1.0)
    return weights, top, total, acc / total


def merge(left, right):
    top = jnp.maximum(left, right)
    w_left, w_right = jnp.exp2(left - top), jnp.exp2(right - top)
    den = w_left + w_right
    return top + jnp.log2(den), w_left / den, w_right / den


def backward_of(i, probs, delta, q, k, v, g, gk, gv):
    query, grad = chunk(q, i), chunk(g, i)
    gq = None
    for j, p in enumerate(probs):
        dv = dot(p.astype(BF16), grad)
        dp = dot_t(chunk(v, j), grad)
        ds = (p * (dp - delta)).astype(BF16)
        dk = dot(ds, query)
        dq = dot_f(chunk(k, j), ds)
        gv[j] = dv if gv[j] is None else gv[j] + dv
        gk[j] = dk if gk[j] is None else gk[j] + dk
        gq = dq if gq is None else gq + dq
    return (gq * SCALE).T


def row_forward_kernel(q_ref, k_ref, v_ref, g_ref, o_ref, lse_ref, dot_ref):
    q, k, v, g = q_ref[0], k_ref[0], v_ref[0], g_ref[0]
    for i in range(q.shape[0] // CHUNK):
        span = slice(i * CHUNK, (i + 1) * CHUNK)
        _, top, total, out = softmax_of(scores_of(chunk(q, i), k, row_bias, i), v)
        o_ref[0, 0, :, span] = out
        lse_ref[0, 0, :, span] = top + jnp.log2(total)
        grad_t = chunk(g, i).astype(F32).T
        dot_ref[0, 0, :, span] = jnp.sum(grad_t * out, axis=0, keepdims=True)


def row_forward(q, k, v, g):
    rows, length, width = q.shape
    heads = width // HEAD_DIM
    block = pl.BlockSpec((1, length, HEAD_DIM), lambda r, h: (r, 0, h))
    stat = pl.BlockSpec((1, 1, 1, length), lambda r, h: (r, h, 0, 0))
    stat_shape = jax.ShapeDtypeStruct((rows, heads, 1, length), F32)
    return pl.pallas_call(
        row_forward_kernel,
        grid=(rows, heads),
        in_specs=[block] * 4,
        out_specs=[
            pl.BlockSpec((1, 1, HEAD_DIM, length), lambda r, h: (r, h, 0, 0)),
            stat,
            stat,
        ],
        out_shape=[
            jax.ShapeDtypeStruct((rows, heads, HEAD_DIM, length), F32),
            stat_shape,
            stat_shape,
        ],
        cost_estimate=pl.CostEstimate(
            flops=rows * heads * length * length * HEAD_DIM * 8,
            bytes_accessed=rows * length * width * 12,
            transcendentals=rows * heads * length * length,
        ),
        name="row_forward",
    )(q, k, v, g)


def col_kernel(x_ref, stat_ref, y_ref, lse_ref):
    devices, _, _, per, width = x_ref.shape
    tokens = devices * per
    chunks = tokens // CHUNK
    q, k, v, g = [x_ref[:, a, 0].reshape(tokens, width) for a in range(4)]
    gk, gv = [None] * chunks, [None] * chunks
    slab = CHUNK // per
    for i in range(chunks):
        span = slice(i * CHUNK, (i + 1) * CHUNK)
        here = slice(i * slab, (i + 1) * slab)
        weights, top, total, out = softmax_of(scores_of(chunk(q, i), k, col_bias, i), v)
        lse_col = top + jnp.log2(total)
        lse_ref[0, 0, :, span] = lse_col
        out_low = out.T.astype(BF16)
        y_ref[here, 0, 0] = out_low.reshape(slab, per, width)
        lse, w_row, w_col = merge(stat_ref[0, 0, 0, :, span], lse_col)
        dot_col = jnp.sum(
            (chunk(g, i).astype(F32) * out_low.astype(F32)).T, axis=0, keepdims=True
        )
        delta = w_row * stat_ref[1, 0, 0, :, span] + w_col * dot_col
        factor = jnp.exp2(top - lse)
        probs = [w * factor for w in weights]
        gq = backward_of(i, probs, delta, q, k, v, g, gk, gv)
        y_ref[here, 1, 0] = gq.astype(BF16).reshape(slab, per, width)
    for j in range(chunks):
        here = slice(j * slab, (j + 1) * slab)
        y_ref[here, 2, 0] = (gk[j] * SCALE).astype(BF16).reshape(slab, per, width)
        y_ref[here, 3, 0] = gv[j].astype(BF16).reshape(slab, per, width)


def col_both(x, stats, first_head):
    devices, kinds, groups, per, width = x.shape
    heads = width // HEAD_DIM
    tokens = devices * per
    block = pl.BlockSpec(
        (devices, kinds, 1, per, HEAD_DIM), lambda c, h: (0, 0, c, 0, h)
    )
    return pl.pallas_call(
        col_kernel,
        grid=(groups, heads),
        in_specs=[
            block,
            pl.BlockSpec((2, 1, 1, 1, tokens), lambda c, h: (0, first_head + h, c, 0, 0)),
        ],
        out_specs=[block, pl.BlockSpec((1, 1, 1, tokens), lambda c, h: (h, c, 0, 0))],
        out_shape=[
            jax.ShapeDtypeStruct(x.shape, BF16),
            jax.ShapeDtypeStruct((heads, groups, 1, tokens), F32),
        ],
        cost_estimate=pl.CostEstimate(
            flops=groups * heads * tokens * tokens * HEAD_DIM * 20,
            bytes_accessed=x.size * 4,
            transcendentals=groups * heads * tokens * tokens,
        ),
        name="col_both",
    )(x, stats)


def row_backward_kernel(
    q_ref, k_ref, v_ref, g_ref, o_ref, lse_ref, back_ref, lse_col_ref, *rest
):
    att_ref, gq_ref, gk_ref, gv_ref = rest[-4:]
    q, k, v, g = q_ref[0], k_ref[0], v_ref[0], g_ref[0]
    length = q.shape[0]
    chunks = length // CHUNK
    devices = back_ref.shape[0]
    slab = devices // chunks

    def came_back(kind, i):
        part = back_ref[i * slab : (i + 1) * slab, kind, :, 0].astype(F32)
        return part.reshape(CHUNK, HEAD_DIM)

    gk, gv = [None] * chunks, [None] * chunks
    for i in range(chunks):
        span = slice(i * CHUNK, (i + 1) * CHUNK)
        lse, w_row, w_col = merge(lse_ref[0, 0, :, span], lse_col_ref[0, 0, :, span])
        col_t = came_back(0, i).T
        att_t = o_ref[0, 0, :, span] * w_row + col_t * w_col
        low = att_t.T.astype(BF16)
        att_ref[0, span, :] = low
        delta = jnp.sum(
            (chunk(g, i).astype(F32) * low.astype(F32)).T, axis=0, keepdims=True
        )
        scores = scores_of(chunk(q, i), k, row_bias, i)
        probs = [jnp.exp2(s - lse) for s in scores]
        gq = backward_of(i, probs, delta, q, k, v, g, gk, gv)
        gq_ref[0, span, :] = (gq + came_back(1, i)).astype(BF16)
    for j in range(chunks):
        span = slice(j * CHUNK, (j + 1) * CHUNK)
        gk_ref[0, span, :] = (gk[j] * SCALE + came_back(2, j)).astype(BF16)
        gv_ref[0, span, :] = (gv[j] + came_back(3, j)).astype(BF16)


def row_backward(q, k, v, g, o, lse, back, lse_col, first_head, earlier):
    rows, length, width = q.shape
    devices, kinds, groups, _, size, piece = back.shape
    heads = piece // HEAD_DIM
    block = pl.BlockSpec((1, length, HEAD_DIM), lambda r, h: (r, 0, first_head + h))
    stat = pl.BlockSpec((1, 1, 1, length), lambda r, h: (r, first_head + h, 0, 0))
    in_specs = [block] * 4 + [
        pl.BlockSpec((1, 1, HEAD_DIM, length), lambda r, h: (r, first_head + h, 0, 0)),
        stat,
        pl.BlockSpec(
            (devices, kinds, groups, 1, size, HEAD_DIM), lambda r, h: (0, 0, 0, r, 0, h)
        ),
        stat,
    ]
    aliases = {}
    if earlier:
        aliases = {len(in_specs) + n: n for n in range(4)}
        in_specs = in_specs + [pl.BlockSpec(memory_space=pl.ANY)] * 4
    return pl.pallas_call(
        row_backward_kernel,
        grid=(rows, heads),
        in_specs=in_specs,
        out_specs=[block] * 4,
        out_shape=[jax.ShapeDtypeStruct(q.shape, BF16)] * 4,
        input_output_aliases=aliases,
        cost_estimate=pl.CostEstimate(
            flops=rows * heads * length * length * HEAD_DIM * 14,
            bytes_accessed=rows * length * piece * 28,
            transcendentals=rows * heads * length * length,
        ),
        name="row_backward",
    )(q, k, v, g, o, lse, back, lse_col, *earlier)


def exchange(array):
    return lax.all_to_all(array, "seq", split_axis=0, concat_axis=0, tiled=True)


def on_device(queries, key_vectors, value_vectors, grad_output):
    devices = lax.axis_size("seq")
    rows = queries.shape[0] // ROW_LEN
    width = queries.shape[1]
    heads = width // HEAD_DIM
    groups = ROW_LEN // devices // GROUP
    per = rows * GROUP
    tokens = devices * per
    piece = width // PIECES
    piece_heads = piece // HEAD_DIM
    arrays = (queries, key_vectors, value_vectors, grad_output)
    by_row = [a.reshape(rows, ROW_LEN, width) for a in arrays]

    packs = []
    for n in range(PIECES):
        parts = [
            jnp.transpose(
                a[:, n * piece : (n + 1) * piece].reshape(rows, devices, groups, GROUP, piece),
                (1, 2, 0, 3, 4),
            )
            for a in arrays
        ]
        packed = jnp.stack(parts, axis=1).reshape(devices, 4, groups, per, piece)
        packs.append(packed)
    arrived = [exchange(packs[0])]

    o, lse, dots = row_forward(*by_row)
    stats = jnp.stack([lse, dots]).reshape(2, rows, heads, devices, groups, GROUP)
    stats = jnp.transpose(stats, (3, 0, 2, 4, 1, 5)).reshape(devices, -1)
    arrived[0], stats = lax.optimization_barrier((arrived[0], stats))
    stats = exchange(stats)
    for n in range(1, PIECES):
        packs[n], stats = lax.optimization_barrier((packs[n], stats))
        arrived.append(exchange(packs[n]))
    stats = stats.reshape(devices, 2, heads, groups, per)
    stats = jnp.transpose(stats, (1, 2, 3, 0, 4)).reshape(2, heads, groups, 1, tokens)

    columns = [col_both(arrived[n], stats, n * piece_heads) for n in range(PIECES)]
    lse_col = jnp.concatenate([lse_col for _, lse_col in columns], axis=0)
    lse_col = jnp.transpose(
        lse_col.reshape(heads, groups, devices, per), (2, 0, 1, 3)
    ).reshape(devices, -1)
    lse_col = exchange(lse_col)
    sent = [y for y, _ in columns]
    sent[-1], lse_col = lax.optimization_barrier((sent[-1], lse_col))
    lse_col = lse_col.reshape(devices, heads, groups, rows, GROUP)
    lse_col = jnp.transpose(lse_col, (3, 1, 0, 2, 4)).reshape(rows, heads, 1, ROW_LEN)
    backs = [exchange(y).reshape(devices, 4, groups, rows, GROUP, piece) for y in sent]

    outs = ()
    for n in range(PIECES):
        outs = row_backward(*by_row, o, lse, backs[n], lse_col, n * piece_heads, tuple(outs))
    return tuple(a.reshape(queries.shape) for a in outs)


def solution(mesh):
    spec = P("seq", "head")
    return jax.shard_map(
        on_device,
        mesh=mesh,
        in_specs=(spec,) * 4,
        out_specs=(spec,) * 4,
        check_vma=False,
    )
```

profile of v0, /device:TPU:14, one launch (start us, length us, event | category | flops | bytes accessed | tf_op | source)
XLA Modules:
  0.0 457.6 jit_solution(1323672938466077204)
XLA Ops:
  0.7 1.8 fusion
  6.7 2.3 pad_maximum_fusion.1
  8.9 7.1 %all-to-all-start = ((bf16[16,4,4,32,256]{4,3,2,1,0:T(8,128)(2,1)}), bf16[16,4,4,32,256]{4,3,2,1,0:T(8,128)(2,1)}, u32[]{:S(2)}, u32[]{:S(2)}) async-start(bf16[16,4,4,32,256]{4,3,2,1,0:T(8,128)(2,1)} %pad_maximum_fusion.1), calls=%async_computation | async-start | bytes 8388608 | tf_op jit(solution)/shard_map/all_to_all | solution.py:269
  16.1 17.4 %row_forward.1 = (f32[4,4,128,512]{3,2,1,0:T(8,128)}, f32[4,4,1,512]{3,2,1,0:T(1,128)}, f32[4,4,1,512]{3,2,1,0:T(1,128)}) custom-call(bf16[4,512,512]{2,1,0:T(8,128)(2,1)} %bitcast.67, bf16[4,512,512]{2,1,0:T(8,128)(2,1)} %bitcast.70, bf16[4,512,512]{2,1,0:T(8,128)(2,1)} %bitcast.73, bf16[4,512,512]{2,1,0:T(8,128)(2,1)} %bitcast.76), custom_call_target="tpu_custom_call" | custom-call | flops 4294967296 | bytes 12582912 | tf_op jit(solution)/shard_map/row_forward/pallas_call | solution.py:118
  35.2 1.4 stack.49
  36.6 1.4 stack.50
  38.1 1.5 maximum_bitcast_fusion
  40.7 2.6 copy_bitcast_fusion.6
  43.2 1.6 copy_bitcast_fusion.4
  44.9 66.0 %all-to-all-done.x_ref = bf16[16,4,4,32,256]{4,3,2,1,0:T(8,128)(2,1)} async-done(((bf16[16,4,4,32,256]{4,3,2,1,0:T(8,128)(2,1)}), bf16[16,4,4,32,256]{4,3,2,1,0:T(8,128)(2,1)}, u32[]{:S(2)}, u32[]{:S(2)}) %all-to-all-start) | async-done | bytes 4194336 | tf_op jit(solution)/shard_map/all_to_all | solution.py:269
  110.8 1.8 copy.45
  112.7 5.1 %all-to-all-start.1 = ((f32[16,1,1024]{2,1,0:T(1,128)}), f32[16,1,1024]{2,1,0:T(1,128)S(1)}, u32[]{:S(2)}, u32[]{:S(2)}) async-start(f32[16,1,1024]{2,1,0:T(1,128)} %copy.45), calls=%async_computation.1 | async-start | bytes 131072 | tf_op jit(solution)/shard_map/all_to_all | solution.py:269
  117.8 3.4 pad_maximum_fusion
  122.4 7.4 %all-to-all-start.2 = ((bf16[16,4,4,32,256]{4,3,2,1,0:T(8,128)(2,1)}), bf16[16,4,4,32,256]{4,3,2,1,0:T(8,128)(2,1)}, u32[]{:S(2)}, u32[]{:S(2)}) async-start(bf16[16,4,4,32,256]{4,3,2,1,0:T(8,128)(2,1)} %pad_maximum_fusion), calls=%async_computation.2 | async-start | bytes 8388608 | tf_op jit(solution)/shard_map/all_to_all | solution.py:269
  130.9 17.4 %col_both.3 = (bf16[16,4,4,32,256]{4,3,2,1,0:T(8,128)(2,1)}, f32[2,4,1,512]{3,2,1,0:T(1,128)}) custom-call(bf16[16,4,4,32,256]{4,3,2,1,0:T(8,128)(2,1)} %all-to-all-done.x_ref, f32[2,4,4,1,512]{4,3,2,1,0:T(1,128)} %reshape.123.stat_ref), custom_call_target="tpu_custom_call" | custom-call | flops 5368709120 | bytes 8388608 | tf_op jit(solution)/shard_map/col_both/pallas_call | solution.py:178
  148.4 72.6 %all-to-all-done.2.x_ref = bf16[16,4,4,32,256]{4,3,2,1,0:T(8,128)(2,1)} async-done(((bf16[16,4,4,32,256]{4,3,2,1,0:T(8,128)(2,1)}), bf16[16,4,4,32,256]{4,3,2,1,0:T(8,128)(2,1)}, u32[]{:S(2)}, u32[]{:S(2)}) %all-to-all-start.2) | async-done | bytes 4194336 | tf_op jit(solution)/shard_map/all_to_all | solution.py:269
  220.9 17.6 %col_both.2 = (bf16[16,4,4,32,256]{4,3,2,1,0:T(8,128)(2,1)}, f32[2,4,1,512]{3,2,1,0:T(1,128)}) custom-call(bf16[16,4,4,32,256]{4,3,2,1,0:T(8,128)(2,1)} %all-to-all-done.2.x_ref, f32[2,4,4,1,512]{4,3,2,1,0:T(1,128)} %reshape.123.stat_ref), custom_call_target="tpu_custom_call" | custom-call | flops 5368709120 | bytes 8388608 | tf_op jit(solution)/shard_map/col_both/pallas_call | solution.py:178
  239.6 9.2 %all_to_all.45 = f32[16,1,512]{2,1,0:T(1,128)S(1)} all-to-all(f32[16,1,512]{2,1,0:T(1,128)S(1)} %all_to_all.38), channel_id=1, replica_groups=mesh['seq'=16,'head'=2] {'seq'}, dimensions={0} | all-to-all | bytes 65536 | tf_op jit(solution)/shard_map/all_to_all | solution.py:269
  248.9 7.5 %all-to-all-start.5 = ((bf16[16,4,4,32,256]{4,3,2,1,0:T(8,128)(2,1)}), bf16[16,4,4,32,256]{4,3,2,1,0:T(8,128)(2,1)}, u32[]{:S(2)}, u32[]{:S(2)}) async-start(bf16[16,4,4,32,256]{4,3,2,1,0:T(8,128)(2,1)} %get-tuple-element.37), calls=%async_computation.5 | async-start | bytes 8388608 | tf_op jit(solution)/shard_map/all_to_all | solution.py:269
  256.5 91.0 %all-to-all-done.5 = bf16[16,4,4,32,256]{4,3,2,1,0:T(8,128)(2,1)} async-done(((bf16[16,4,4,32,256]{4,3,2,1,0:T(8,128)(2,1)}), bf16[16,4,4,32,256]{4,3,2,1,0:T(8,128)(2,1)}, u32[]{:S(2)}, u32[]{:S(2)}) %all-to-all-start.5) | async-done | bytes 4194336 | tf_op jit(solution)/shard_map/all_to_all | solution.py:269
  347.5 5.1 %all-to-all-start.4 = ((bf16[16,4,4,32,256]{4,3,2,1,0:T(8,128)(2,1)}), bf16[16,4,4,32,256]{4,3,2,1,0:T(8,128)(2,1)}, u32[]{:S(2)}, u32[]{:S(2)}) async-start(bf16[16,4,4,32,256]{4,3,2,1,0:T(8,128)(2,1)} %get-tuple-element.35), calls=%async_computation.4 | async-start | bytes 8388608 | tf_op jit(solution)/shard_map/all_to_all | solution.py:269
  354.0 12.3 %row_backward.2 = (bf16[4,512,512]{2,1,0:T(8,128)(2,1)}, bf16[4,512,512]{2,1,0:T(8,128)(2,1)}, bf16[4,512,512]{2,1,0:T(8,128)(2,1)}, bf16[4,512,512]{2,1,0:T(8,128)(2,1)}) custom-call(bf16[4,512,512]{2,1,0:T(8,128)(2,1)} %bitcast.68, bf16[4,512,512]{2,1,0:T(8,128)(2,1)} %bitcast.71, bf16[4,512,512]{2,1,0:T(8,128)(2,1)} %bitcast.74, ...), custom_call_target="tpu_custom_call" | custom-call | flops 3758096384 | bytes 14680064 | tf_op jit(solution)/shard_map/row_backward/pallas_call | solution.py:252
  366.3 78.9 %all-to-all-done.4 = bf16[16,4,4,32,256]{4,3,2,1,0:T(8,128)(2,1)} async-done(((bf16[16,4,4,32,256]{4,3,2,1,0:T(8,128)(2,1)}), bf16[16,4,4,32,256]{4,3,2,1,0:T(8,128)(2,1)}, u32[]{:S(2)}, u32[]{:S(2)}) %all-to-all-start.4) | async-done | bytes 4194336 | tf_op jit(solution)/shard_map/all_to_all | solution.py:269
  445.2 12.2 %row_backward.3 = (bf16[4,512,512]{2,1,0:T(8,128)(2,1)}, bf16[4,512,512]{2,1,0:T(8,128)(2,1)}, bf16[4,512,512]{2,1,0:T(8,128)(2,1)}, bf16[4,512,512]{2,1,0:T(8,128)(2,1)}) custom-call(bf16[4,512,512]{2,1,0:T(8,128)(2,1)} %bitcast.69, bf16[4,512,512]{2,1,0:T(8,128)(2,1)} %bitcast.72, ...), custom_call_target="tpu_custom_call", output_to_operand_aliasing={{0}: (8, {}), {1}: (9, {}), {2}: (10, {}), {3}: (11, {})} | custom-call | flops 3758096384 | bytes 14680064 | tf_op jit(solution)/shard_map/row_backward/pallas_call | solution.py:252
  (32 shorter events, 11.9 us)
Async XLA Ops:
  0.6 2.2 copy-start
  0.6 3.3 copy-start.1
  2.9 2.1 copy-start.2
  8.9 101.9 %all-to-all-start = ((bf16[16,4,4,32,256]{4,3,2,1,0:T(8,128)(2,1)}), bf16[16,4,4,32,256]{4,3,2,1,0:T(8,128)(2,1)}, u32[]{:S(2)}, u32[]{:S(2)}) async-start(bf16[16,4,4,32,256]{4,3,2,1,0:T(8,128)(2,1)} %pad_maximum_fusion.1), calls=%async_computation | async-start | bytes 8388608 | tf_op jit(solution)/shard_map/all_to_all | solution.py:269
  40.7 2.6 copy-start.3
  43.2 74.6 %copy-start.4 = (bf16[16,1,4,32,256]{4,3,2,1,0:T(8,128)(2,1)S(1)}, bf16[16,1,4,32,256]{4,3,2,1,0:T(8,128)(2,1)}, u32[]{:S(2)}) copy-start(bf16[16,1,4,32,256]{4,3,2,1,0:T(8,128)(2,1)} %get-tuple-element.57) | copy-start | bytes 3145732
  112.7 9.7 %all-to-all-start.1 = ((f32[16,1,1024]{2,1,0:T(1,128)}), f32[16,1,1024]{2,1,0:T(1,128)S(1)}, u32[]{:S(2)}, u32[]{:S(2)}) async-start(f32[16,1,1024]{2,1,0:T(1,128)} %copy.45), calls=%async_computation.1 | async-start | bytes 131072 | tf_op jit(solution)/shard_map/all_to_all | solution.py:269
  122.4 98.6 %all-to-all-start.2 = ((bf16[16,4,4,32,256]{4,3,2,1,0:T(8,128)(2,1)}), bf16[16,4,4,32,256]{4,3,2,1,0:T(8,128)(2,1)}, u32[]{:S(2)}, u32[]{:S(2)}) async-start(bf16[16,4,4,32,256]{4,3,2,1,0:T(8,128)(2,1)} %pad_maximum_fusion), calls=%async_computation.2 | async-start | bytes 8388608 | tf_op jit(solution)/shard_map/all_to_all | solution.py:269
  148.4 90.1 %copy-start.5 = (f32[2,4,1,512]{3,2,1,0:T(1,128)S(1)}, f32[2,4,1,512]{3,2,1,0:T(1,128)}, u32[]{:S(2)}) copy-start(f32[2,4,1,512]{3,2,1,0:T(1,128)} %get-tuple-element.33) | copy-start | bytes 49156
  248.9 98.6 %all-to-all-start.5 = ((bf16[16,4,4,32,256]{4,3,2,1,0:T(8,128)(2,1)}), bf16[16,4,4,32,256]{4,3,2,1,0:T(8,128)(2,1)}, u32[]{:S(2)}, u32[]{:S(2)}) async-start(bf16[16,4,4,32,256]{4,3,2,1,0:T(8,128)(2,1)} %get-tuple-element.37), calls=%async_computation.5 | async-start | bytes 8388608 | tf_op jit(solution)/shard_map/all_to_all | solution.py:269
  347.5 97.7 %all-to-all-start.4 = ((bf16[16,4,4,32,256]{4,3,2,1,0:T(8,128)(2,1)}), bf16[16,4,4,32,256]{4,3,2,1,0:T(8,128)(2,1)}, u32[]{:S(2)}, u32[]{:S(2)}) async-start(bf16[16,4,4,32,256]{4,3,2,1,0:T(8,128)(2,1)} %get-tuple-element.35), calls=%async_computation.4 | async-start | bytes 8388608 | tf_op jit(solution)/shard_map/all_to_all | solution.py:269
where the time goes:
time: 459 us; the launch traced here: 458 us
  waiting for transfers between devices  310 us (68%)
  Pallas kernels  76.9 us (17%)
  starting transfers between devices  32.3 us (7%)
  local copies, waits for them, and re-layouts  19 us (4%)
  other arithmetic  9.65 us (2%)
  blocking collectives  9.23 us (2%)
    all_to_all x5, waiting for transfers between devices, exchange(): return lax.all_to_all(array, 'seq', split_axis=0, concat_axis=0, tiled=True)  310 us
    pallas_call x2, Pallas kernels, col_both(): pl.pallas_call(col_kernel, grid=(groups, heads), in_specs=[block, pl.Bloc...  35 us
    all_to_all x5, starting transfers between devices, exchange(): return lax.all_to_all(array, 'seq', split_axis=0, concat_axis=0, tiled=True)  32.3 us
    pallas_call x2, Pallas kernels, row_backward(): pl.pallas_call(row_backward_kernel, grid=(rows, heads), in_specs=in_specs...  24.5 us
    pallas_call x1, Pallas kernels, row_forward(): pl.pallas_call(row_forward_kernel, grid=(rows, heads), in_specs=[block] *...  17.4 us
    all_to_all x1, blocking collectives, exchange(): return lax.all_to_all(array, 'seq', split_axis=0, concat_axis=0, tiled=True)  9.23 us
  transfers between devices with their start and end apart: 5, of which 5 were waited for; matrix products, arithmetic and copies ran while one was open for 4% of the time, Pallas kernels for 10%

commit v1 on v0

--- a/solution.py
+++ b/solution.py
@@ -269,7 +269,7 @@
     return lax.all_to_all(array, "seq", split_axis=0, concat_axis=0, tiled=True)
 
 
-def on_device(queries, key_vectors, value_vectors, grad_output):
+def by_all_to_all(queries, key_vectors, value_vectors, grad_output):
     devices = lax.axis_size("seq")
     rows = queries.shape[0] // ROW_LEN
     width = queries.shape[1]
@@ -324,6 +324,507 @@
     return tuple(a.reshape(queries.shape) for a in outs)
 
 
+PLANES = 4
+SPLITS = 4
+LANES = 128
+
+
+def drain(ref, sem):
+    pltpu.make_async_copy(ref, ref, sem).wait()
+
+
+def fold_lanes(x):
+    for shift in (8, 16, 32, 64):
+        x = x + pltpu.roll(x, shift, 1)
+    return x
+
+
+def lane_masks():
+    group = lax.broadcasted_iota(jnp.int32, (LANES // GROUP, LANES), 1) // GROUP
+    row = lax.broadcasted_iota(jnp.int32, (LANES // GROUP, LANES), 0)
+    return group, group == row
+
+
+def to_tile(stat, block):
+    group, diagonal = lane_masks()
+    spread = fold_lanes(jnp.where(group == block, stat, 0.0))
+    return jnp.sum(jnp.where(diagonal, spread, 0.0), axis=0, keepdims=True)
+
+
+def from_tile(line, block):
+    group, diagonal = lane_masks()
+    spread = fold_lanes(jnp.where(diagonal, line, 0.0))
+    return jnp.where(group == block, spread, 0.0)
+
+
+def column_unit(q, g, keys, values, query_chunk, lse_row, dot_row):
+    count = len(keys)
+    scores = []
+    for j in range(count):
+        bias = col_bias(None, j, count - 1)
+        scores.append(dot_t(keys[j], q) * (SCALE * LOG2E) + bias)
+    top = functools.reduce(
+        jnp.maximum, [jnp.max(s, axis=0, keepdims=True) for s in scores]
+    )
+    top = jnp.maximum(top, FLOOR)
+    weights = [jnp.exp2(s - top) for s in scores]
+    total = sum(jnp.sum(w, axis=0, keepdims=True) for w in weights)
+    acc = sum(dot_f(v, w.astype(BF16)) for v, w in zip(values, weights))
+    total = jnp.maximum(total, 1.0)
+    out_low = (acc / total).T.astype(BF16)
+    lse_col = top + jnp.log2(total)
+    lse, w_row, w_col = merge(lse_row, lse_col)
+    dot_col = jnp.sum(
+        (g.astype(F32) * out_low.astype(F32)).T, axis=0, keepdims=True
+    )
+    delta = w_row * dot_row + w_col * dot_col
+    factor = jnp.exp2(top - lse)
+    gq, gk, gv = None, [], []
+    for j in range(count):
+        p = weights[j] * factor
+        gv.append(dot(p.astype(BF16), g))
+        dp = dot_t(values[j], g)
+        ds = (p * (dp - delta)).astype(BF16)
+        gk.append(dot(ds, q) * SCALE)
+        dq = dot_f(keys[j], ds)
+        gq = dq if gq is None else gq + dq
+    return out_low, (gq * SCALE).T.astype(BF16), gk, gv, lse_col
+
+
+def fused_kernel(*refs):
+    xs, flat, outs = refs[0:4], refs[4:8], refs[8:12]
+    (xin, own, far, low, back, orow, st_row, st_own, st_far, lse_own, lse_far,
+     lse_back, in_sem, a_loc, a_send, a_recv, b_send, bkv_recv, bqg_recv,
+     k1_send, k1_recv, k0_send, k0_recv, d2_send, d2_recv, d1_send, d1_recv,
+     e_send, e_recv, s_send, s_recv, sf_send, sf_recv, l1_send, l1_recv,
+     le_send, le_recv, out_sem) = refs[12:]
+    heads, _, rows = xin.shape[:3]
+    chunks = own.shape[0]
+    plane_rows, per = own.shape[2], own.shape[3]
+    splits = chunks // heads
+    devices = lax.axis_size("seq")
+    m = devices // PLANES
+    blocks = per * splits
+    seq, head_index = lax.axis_index("seq"), lax.axis_index("head")
+    z, p = seq // m, seq % m
+    first = z * m
+
+    def send(src, dst, send_sem, recv_sem, to):
+        pltpu.make_async_remote_copy(
+            src_ref=src, dst_ref=dst, send_sem=send_sem, recv_sem=recv_sem,
+            device_id=(to, head_index), device_id_type=pl.DeviceIdType.MESH,
+        ).start()
+
+    outer = (z == 0) | (z == PLANES - 1)
+    inner_peer = jnp.where(z == 0, seq + m, seq - m)
+    outer_peer = jnp.where(z == 1, seq - m, seq + m)
+
+    barrier = pltpu.get_barrier_semaphore()
+    for d in range(1, m):
+        pl.semaphore_signal(barrier, inc=1, device_id=(first + (p + d) % m, head_index),
+                            device_id_type=pl.DeviceIdType.MESH)
+    for d in range(1, PLANES):
+        pl.semaphore_signal(barrier, inc=1,
+                            device_id=((z + d) % PLANES * m + p, head_index),
+                            device_id_type=pl.DeviceIdType.MESH)
+
+    def lanes_of(h):
+        return pl.ds(pl.multiple_of(h * HEAD_DIM, HEAD_DIM), HEAD_DIM)
+
+    def load_rows(h, carry):
+        for kind in range(4):
+            pltpu.make_async_copy(
+                flat[kind].at[:, :, lanes_of(h)], xin.at[h, kind], in_sem.at[h]
+            ).start()
+        return carry
+
+    load_rows(0, 0)
+    pl.semaphore_wait(barrier, m - 1 + PLANES - 1)
+
+    def spread_chunk(c, carry):
+        h, part = c // splits, c % splits
+        for d in range(1, m):
+            peer = (p + d) % m
+            for kind in range(4):
+                send(
+                    xs[kind].at[:, pl.ds(peer * blocks + part * per, per), :, lanes_of(h)],
+                    own.at[c, kind, pl.ds(p * rows, rows)],
+                    a_send, a_recv.at[c], first + peer,
+                )
+        for kind in range(4):
+            pltpu.make_async_copy(
+                xs[kind].at[:, pl.ds(p * blocks + part * per, per), :, lanes_of(h)],
+                own.at[c, kind, pl.ds(p * rows, rows)],
+                a_loc.at[c],
+            ).start()
+        return carry
+
+    lax.fori_loop(0, chunks, spread_chunk, 0)
+    lax.fori_loop(1, heads, load_rows, 0)
+
+    def forward_row(h, r):
+        q, k, v, g = [xin[h, kind, r] for kind in range(4)]
+        for i in range(q.shape[0] // CHUNK):
+            span = slice(i * CHUNK, (i + 1) * CHUNK)
+            _, top, total, out = softmax_of(scores_of(chunk(q, i), k, row_bias, i), v)
+            orow[h, r, :, span] = out
+            lse = top + jnp.log2(total)
+            grad_t = chunk(g, i).astype(F32).T
+            dots = jnp.sum(grad_t * out, axis=0, keepdims=True)
+            for part in range(CHUNK // LANES):
+                lanes = slice(part * LANES, (part + 1) * LANES)
+                at = i * (CHUNK // LANES) + part
+                st_row[2 * h, at, pl.ds(r, 1), :] = lse[:, lanes]
+                st_row[2 * h + 1, at, pl.ds(r, 1), :] = dots[:, lanes]
+
+    def forward_head(h):
+        drain(xin.at[h], in_sem.at[h])
+
+        def body(r, carry):
+            forward_row(h, r)
+            return carry
+
+        lax.fori_loop(0, rows, body, 0)
+
+    def send_stats():
+        for d in range(1, m):
+            peer = (p + d) % m
+            send(st_row.at[:, peer], st_own.at[:, p], s_send, s_recv, first + peer)
+        st_own[:, p] = st_row[:, p]
+
+        @pl.when(outer)
+        def _():
+            drain(st_own.at[:, pl.ds(0, m - 1)], s_recv)
+            send(st_own, st_far, sf_send, sf_recv, inner_peer)
+
+    def wait_stats():
+        drain(st_own.at[:, pl.ds(0, m - 1)], s_recv)
+        drain(st_far, sf_recv)
+
+    def tile(ref, *at):
+        return ref[at].reshape(plane_rows * GROUP, HEAD_DIM)
+
+    def put(ref, at, value):
+        ref[at] = value.astype(BF16).reshape(plane_rows, GROUP, HEAD_DIM)
+
+    def stat_of(ref, which, block):
+        return to_tile(ref[which].reshape(plane_rows, LANES), block)
+
+    def add_lse(ref, h, line, block):
+        ref[h] = ref[h] + from_tile(line, block).reshape(m, rows, LANES)
+
+    half = plane_rows * GROUP
+
+    def solve(c, lower):
+        h, part = c // splits, c % splits
+        pair = (far, own) if lower else (own, far)
+        lses = (lse_far, lse_own) if lower else (lse_own, lse_far)
+        stats = (st_far, st_own) if lower else (st_own, st_far)
+
+        @pl.when(part == 0)
+        def _():
+            lse_own[h] = jnp.zeros(lse_own.shape[1:], F32)
+            lse_far[h] = jnp.zeros(lse_far.shape[1:], F32)
+
+        def body(b, carry):
+            block = part * per + b
+            every = slice(None)
+
+            def both(kind):
+                return jnp.concatenate([tile(ref, c, kind, every, b) for ref in pair], axis=0)
+
+            q, k, v, g = [both(kind) for kind in range(4)]
+            keys, values = [k], [v]
+            if not lower:
+                keys = [jnp.concatenate([tile(low, c, 0, every, b), tile(low, c, 2, every, b)], axis=0), k]
+                values = [jnp.concatenate([tile(low, c, 1, every, b), tile(low, c, 3, every, b)], axis=0), v]
+            lse_row = jnp.concatenate([stat_of(s, 2 * h, block) for s in stats], axis=1)
+            dot_row = jnp.concatenate([stat_of(s, 2 * h + 1, block) for s in stats], axis=1)
+            o, gq, gk, gv, lse_col = column_unit(q, g, keys, values, None, lse_row, dot_row)
+            gk_own, gv_own = gk[-1], gv[-1]
+            if lower:
+                gk_own = gk_own + jnp.concatenate(
+                    [tile(low, c, 0, every, b), tile(low, c, 2, every, b)], axis=0).astype(F32)
+                gv_own = gv_own + jnp.concatenate(
+                    [tile(low, c, 1, every, b), tile(low, c, 3, every, b)], axis=0).astype(F32)
+            else:
+                put(low, (c, 0, every, b), gk[0][:half])
+                put(low, (c, 1, every, b), gv[0][:half])
+                put(low, (c, 2, every, b), gk[0][half:])
+                put(low, (c, 3, every, b), gv[0][half:])
+            for n, ref in enumerate(pair):
+                span = slice(n * half, (n + 1) * half)
+                for kind, value in enumerate((o, gq, gk_own, gv_own)):
+                    put(ref, (c, kind, every, b), value[span])
+                add_lse(lses[n], h, lse_col[:, span], block)
+            return carry
+
+        lax.fori_loop(0, per, body, 0)
+
+    def return_rows(c, ref):
+        h, part = c // splits, c % splits
+        at = pl.ds(p * blocks + part * per, per)
+        for d in range(1, m):
+            peer = (p + d) % m
+            send(
+                ref.at[c, :, pl.ds(peer * rows, rows)], back.at[h, :, :, at],
+                e_send, e_recv.at[h], first + peer,
+            )
+        back[h, :, :, at] = ref[c, :, pl.ds(p * rows, rows)]
+
+        @pl.when(part == splits - 1)
+        def _():
+            for d in range(1, m):
+                peer = (p + d) % m
+                send(lse_own.at[h, peer], lse_back.at[h, p], le_send, le_recv.at[h], first + peer)
+            lse_back[h, p] = lse_own[h, p]
+
+    def return_far(c):
+        h, part = c // splits, c % splits
+        send(far.at[c], far.at[c], d1_send, d1_recv.at[c], outer_peer)
+
+        @pl.when(part == splits - 1)
+        def _():
+            send(lse_far.at[h], lse_own.at[h], l1_send, l1_recv.at[h], outer_peer)
+
+    def pass_on(c):
+        drain(own.at[c, :, pl.ds(0, rows * (m - 1))], a_recv.at[c])
+        drain(own.at[c, :, pl.ds(0, rows)], a_loc.at[c])
+
+        @pl.when(outer)
+        def _():
+            send(own.at[c, pl.ds(1, 2)], far.at[c, pl.ds(1, 2)], b_send, bkv_recv.at[c], inner_peer)
+            send(own.at[c, 0], far.at[c, 0], b_send, bqg_recv.at[c, 0], inner_peer)
+            send(own.at[c, 3], far.at[c, 3], b_send, bqg_recv.at[c, 1], inner_peer)
+
+        @pl.when(z == 1)
+        def _():
+            send(own.at[c, pl.ds(1, 2)], low.at[c, pl.ds(2, 2)], k1_send.at[c], k1_recv.at[c], seq + m)
+
+    def pass_far(c):
+        drain(far.at[c, pl.ds(1, 2)], bkv_recv.at[c])
+        send(far.at[c, pl.ds(1, 2)], low.at[c, pl.ds(0, 2)], k0_send.at[c], k0_recv.at[c], seq + m)
+
+    def wait_qg(c):
+        drain(far.at[c, 0], bqg_recv.at[c, 0])
+        drain(far.at[c, 3], bqg_recv.at[c, 1])
+
+    def upper(c):
+        drain(far.at[c, pl.ds(1, 2)], bkv_recv.at[c])
+        wait_qg(c)
+        drain(low.at[c, pl.ds(2, 2)], k1_recv.at[c])
+        drain(low.at[c, pl.ds(0, 2)], k0_recv.at[c])
+        solve(c, False)
+        send(low.at[c], low.at[c], d2_send, d2_recv.at[c], seq - m)
+        return_far(c)
+        return_rows(c, own)
+
+    def lower(c):
+        wait_qg(c)
+        drain(low.at[c], d2_recv.at[c])
+        drain(own.at[c, pl.ds(1, 2)], k1_send.at[c])
+        drain(far.at[c, pl.ds(1, 2)], k0_send.at[c])
+        solve(c, True)
+        return_far(c)
+        return_rows(c, own)
+
+    def edge(c):
+        h, part = c // splits, c % splits
+        drain(far.at[c], d1_recv.at[c])
+
+        @pl.when(part == splits - 1)
+        def _():
+            drain(lse_own.at[h], l1_recv.at[h])
+
+        return_rows(c, far)
+
+    def backward_row(h, r):
+        q, k, v, g = [xin[h, kind, r] for kind in range(4)]
+        count = q.shape[0] // CHUNK
+        slab = CHUNK // GROUP
+
+        def came_back(kind, i):
+            return back[h, kind, r, i * slab:(i + 1) * slab].reshape(CHUNK, HEAD_DIM).astype(F32)
+
+        def give(kind, i, value):
+            back[h, kind, r, i * slab:(i + 1) * slab] = value.astype(BF16).reshape(slab, GROUP, HEAD_DIM)
+
+        def line(ref, lead, i):
+            base = i * (CHUNK // LANES)
+            return jnp.concatenate(
+                [ref[lead, base + n, pl.ds(r, 1), :] for n in range(CHUNK // LANES)], axis=1)
+
+        gk, gv = [None] * count, [None] * count
+        for i in range(count):
+            span = slice(i * CHUNK, (i + 1) * CHUNK)
+            lse, w_row, w_col = merge(line(st_row, 2 * h, i), line(lse_back, h, i))
+            att_t = orow[h, r, :, span] * w_row + came_back(0, i).T * w_col
+            att = att_t.T.astype(BF16)
+            give(0, i, att)
+            delta = jnp.sum(
+                (chunk(g, i).astype(F32) * att.astype(F32)).T, axis=0, keepdims=True
+            )
+            scores = scores_of(chunk(q, i), k, row_bias, i)
+            probs = [jnp.exp2(s - lse) for s in scores]
+            gq = backward_of(i, probs, delta, q, k, v, g, gk, gv)
+            give(1, i, gq + came_back(1, i))
+        for j in range(count):
+            give(2, j, gk[j] * SCALE + came_back(2, j))
+            give(3, j, gv[j] + came_back(3, j))
+
+    def backward_head(h):
+        drain(back.at[h, :, :, pl.ds(0, blocks * (m - 1))], e_recv.at[h])
+        drain(lse_back.at[h, pl.ds(0, m - 1)], le_recv.at[h])
+
+        def body(r, carry):
+            backward_row(h, r)
+            return carry
+
+        lax.fori_loop(0, rows, body, 0)
+        for kind in range(4):
+            pltpu.make_async_copy(
+                back.at[h, kind], outs[kind].at[:, :, :, lanes_of(h)], out_sem
+            ).start()
+
+    lag_upper, lag_lower, lag_edge, lag_rows = LAGS
+
+    def step(s, carry):
+        def at(lag, role=None):
+            ready = (s >= lag) & (s < chunks + lag)
+            return ready if role is None else ready & role
+
+        @pl.when(s < heads)
+        def _():
+            forward_head(s)
+
+        @pl.when(s == heads - 1)
+        def _():
+            send_stats()
+
+        @pl.when(at(0))
+        def _():
+            pass_on(s)
+
+        @pl.when(at(1, z == 1))
+        def _():
+            pass_far(s - 1)
+
+        @pl.when((s == lag_upper) & ((z == 1) | (z == 2)))
+        def _():
+            wait_stats()
+
+        @pl.when(at(lag_upper, z == 2))
+        def _():
+            upper(s - lag_upper)
+
+        @pl.when(at(lag_lower, z == 1))
+        def _():
+            lower(s - lag_lower)
+
+        @pl.when(at(lag_edge, outer))
+        def _():
+            edge(s - lag_edge)
+
+        done = s - lag_rows
+
+        @pl.when((done >= 0) & (done % splits == splits - 1))
+        def _():
+            backward_head(done // splits)
+
+        return carry
+
+    lax.fori_loop(0, chunks + lag_rows, step, 0)
+
+    drain(own.at[:, :, pl.ds(0, rows * (m - 1))], a_send)
+    drain(own.at[:, :, pl.ds(0, rows * (m - 1))], e_send)
+    drain(st_own.at[:, pl.ds(0, m - 1)], s_send)
+    drain(lse_own.at[:, pl.ds(0, m - 1)], le_send)
+
+    @pl.when(outer)
+    def _():
+        drain(own, b_send)
+        drain(st_far, sf_send)
+
+    @pl.when((z == 1) | (z == 2))
+    def _():
+        drain(far, d1_send)
+        drain(lse_far, l1_send)
+
+    @pl.when(z == 2)
+    def _():
+        drain(low, d2_send)
+
+    drain(back, out_sem)
+
+
+LAGS = (3, 6, 8, 11)
+
+
+def fits(tokens, width, devices):
+    rows = tokens // ROW_LEN
+    if tokens % ROW_LEN or devices % PLANES or width % HEAD_DIM:
+        return False
+    m = devices // PLANES
+    blocks = ROW_LEN // GROUP
+    return (
+        m > 1
+        and ROW_LEN // m == LANES
+        and rows * m * GROUP == LANES
+        and (blocks // m) % SPLITS == 0
+    )
+
+
+def by_planes(queries, key_vectors, value_vectors, grad_output):
+    devices = lax.axis_size("seq")
+    m = devices // PLANES
+    tokens, width = queries.shape
+    rows, heads, blocks = tokens // ROW_LEN, width // HEAD_DIM, ROW_LEN // GROUP
+    per = blocks // m // SPLITS
+    chunks = heads * SPLITS
+    arrays = (queries, key_vectors, value_vectors, grad_output)
+    views = [a.reshape(rows, blocks, GROUP, width) for a in arrays]
+    flat = [a.reshape(rows, ROW_LEN, width) for a in arrays]
+    buffer = pltpu.VMEM((chunks, 4, rows * m, per, GROUP, HEAD_DIM), BF16)
+    dma = pltpu.SemaphoreType.DMA
+    stat = pltpu.VMEM((2 * heads, m, rows, LANES), F32)
+    lse = pltpu.VMEM((heads, m, rows, LANES), F32)
+    each, single = dma((chunks,)), dma(())
+    outs = pl.pallas_call(
+        fused_kernel,
+        in_specs=[pl.BlockSpec(memory_space=pl.ANY)] * 8,
+        out_specs=[pl.BlockSpec(memory_space=pl.ANY)] * 4,
+        out_shape=[jax.ShapeDtypeStruct(views[0].shape, BF16)] * 4,
+        scratch_shapes=[
+            pltpu.VMEM((heads, 4, rows, ROW_LEN, HEAD_DIM), BF16),
+            buffer, buffer, buffer,
+            pltpu.VMEM((heads, 4, rows, blocks, GROUP, HEAD_DIM), BF16),
+            pltpu.VMEM((heads, rows, HEAD_DIM, ROW_LEN), F32),
+            stat, stat, stat, lse, lse, lse,
+            dma((heads,)), each, single, each, single, each, dma((chunks, 2)),
+            each, each, each, each, single, each, single, each,
+            single, dma((heads,)), single, single, single, single, single, dma((heads,)),
+            single, dma((heads,)), single,
+        ],
+        compiler_params=pltpu.CompilerParams(
+            collective_id=0, has_side_effects=True, vmem_limit_bytes=63 * 1024 * 1024
+        ),
+        cost_estimate=pl.CostEstimate(
+            flops=tokens * width * 512 * 24,
+            bytes_accessed=tokens * width * 16,
+            transcendentals=tokens * width,
+        ),
+        name="by_planes",
+    )(*views, *flat)
+    return tuple(a.reshape(queries.shape) for a in outs)
+
+
+def on_device(queries, key_vectors, value_vectors, grad_output):
+    arrays = (queries, key_vectors, value_vectors, grad_output)
+    if fits(*queries.shape, lax.axis_size("seq")):
+        return by_planes(*arrays)
+    return by_all_to_all(*arrays)
+
+
 def solution(mesh):
     spec = P("seq", "head")
     return jax.shard_map(

time: 459 us -> 336 us (0.73)
  the two profiles are of different devices: /device:TPU:14 before, /device:TPU:0 now
where the time goes in v1:
time: 336 us
  Pallas kernels  326 us (97%)
  local copies, waits for them, and re-layouts  9.21 us (3%)
    pallas_call x1, Pallas kernels, by_planes(): pl.pallas_call(fused_kernel, in_specs=[pl.BlockSpec(memory_space=pl.ANY)]...  326 us
    unnamed x10, local copies, waits for them, and re-layouts  9.21 us

profile of v1, /device:TPU:0, one launch (start us, length us, event | category | flops | bytes accessed | tf_op | source)
XLA Modules:
  0.0 335.8 jit_solution(5435834599891924415)
XLA Ops:
  0.6 325.9 %by_planes.1 = (bf16[4,64,8,512]{3,2,1,0:T(8,128)(2,1)}, bf16[4,64,8,512]{3,2,1,0:T(8,128)(2,1)}, bf16[4,64,8,512]{3,2,1,0:T(8,128)(2,1)}, bf16[4,64,8,512]{3,2,1,0:T(8,128)(2,1)}) custom-call(bf16[4,64,8,512]{3,2,1,0:T(8,128)(2,1)} %bitcast.16, bf16[4,64,8,512]{3,2,1,0:T(8,128)(2,1)} %bitcast.18, bf16[4,64,8,512]{3,2,1,0:T(8,128)(2,1)} %bitcast.20, ...), custom_call_target="tpu_custom_call" | custom-call | flops 12884901888 | bytes 16777216 | tf_op jit(solution)/shard_map/by_planes/pallas_call | solution.py:792
  326.5 0.0 copy-start.2
  326.5 3.2 copy.12
  329.7 0.0 copy-done.2
  329.7 0.0 copy-start.1
  329.7 1.3 copy.13
  331.1 1.0 copy-done.1
  332.1 0.0 copy-start
  332.1 1.3 copy.14
  333.4 1.0 copy-done
  334.4 1.3 copy.15
Async XLA Ops:
  326.5 3.2 copy-start.2
  329.7 2.3 copy-start.1
  332.1 2.3 copy-start

commit v2 on v1

--- a/solution.py
+++ b/solution.py
@@ -325,7 +325,7 @@
 
 
 PLANES = 4
-SPLITS = 4
+SPLITS = 16
 LANES = 128
 
 
@@ -459,7 +459,7 @@
             ).start()
         return carry
 
-    lax.fori_loop(0, chunks, spread_chunk, 0)
+    lax.fori_loop(0, AHEAD, spread_chunk, 0)
     lax.fori_loop(1, heads, load_rows, 0)
 
     def forward_row(h, r):
@@ -705,6 +705,10 @@
         def _():
             pass_on(s)
 
+        @pl.when(s + AHEAD < chunks)
+        def _():
+            spread_chunk(s + AHEAD, 0)
+
         @pl.when(at(1, z == 1))
         def _():
             pass_far(s - 1)
@@ -757,6 +761,7 @@
     drain(back, out_sem)
 
 
+AHEAD = 2
 LAGS = (3, 6, 8, 11)
 
 

time: 336 us -> 244 us (0.73)
  Pallas kernels: 326 us -> 234 us
    pallas_call x1, Pallas kernels: 326 us -> 234 us  [by_planes(): pl.pallas_call(fused_kernel, in_specs=[pl.BlockSpec(memory_space=pl.ANY)]...]
where the time goes in v2:
time: 244 us
  Pallas kernels  234 us (96%)
  local copies, waits for them, and re-layouts  9.21 us (4%)
    pallas_call x1, Pallas kernels, by_planes(): pl.pallas_call(fused_kernel, in_specs=[pl.BlockSpec(memory_space=pl.ANY)]...  234 us
    unnamed x10, local copies, waits for them, and re-layouts  9.21 us

profile of v2, /device:TPU:0, one launch (start us, length us, event | category | flops | bytes accessed | tf_op | source)
XLA Modules:
  0.0 244.1 jit_solution(1163203272262975856)
XLA Ops:
  0.6 234.3 %by_planes.1 = (bf16[4,64,8,512]{3,2,1,0:T(8,128)(2,1)}, bf16[4,64,8,512]{3,2,1,0:T(8,128)(2,1)}, bf16[4,64,8,512]{3,2,1,0:T(8,128)(2,1)}, bf16[4,64,8,512]{3,2,1,0:T(8,128)(2,1)}) custom-call(bf16[4,64,8,512]{3,2,1,0:T(8,128)(2,1)} %bitcast.16, bf16[4,64,8,512]{3,2,1,0:T(8,128)(2,1)} %bitcast.18, bf16[4,64,8,512]{3,2,1,0:T(8,128)(2,1)} %bitcast.20, ...), custom_call_target="tpu_custom_call" | custom-call | flops 12884901888 | bytes 16777216 | tf_op jit(solution)/shard_map/by_planes/pallas_call | solution.py:797
  234.9 0.0 copy-start.2
  234.9 3.2 %copy.12 = bf16[2048,512]{1,0:T(8,128)(2,1)} copy(bf16[2048,512]{1,0:T(8,128)(2,1)} %bitcast.15) | data formatting | bytes 4194304
  238.1 0.0 copy-done.2
  238.1 0.0 copy-start.1
  238.1 1.3 copy.13
  239.4 1.0 copy-done.1
  240.5 0.0 copy-start
  240.5 1.3 copy.14
  241.8 1.0 copy-done
  242.8 1.3 copy.15
Async XLA Ops:
  234.9 3.2 %copy-start.2 = (bf16[4,64,8,512]{3,2,1,0:T(8,128)(2,1)S(1)}, bf16[4,64,8,512]{3,2,1,0:T(8,128)(2,1)}, u32[]{:S(2)}) copy-start(bf16[4,64,8,512]{3,2,1,0:T(8,128)(2,1)} %get-tuple-element.9) | copy-start | bytes 6291460
  238.1 2.3 copy-start.1
  240.5 2.3 copy-start

commit v3 on v2

--- a/solution.py
+++ b/solution.py
@@ -477,29 +477,20 @@
                 st_row[2 * h, at, pl.ds(r, 1), :] = lse[:, lanes]
                 st_row[2 * h + 1, at, pl.ds(r, 1), :] = dots[:, lanes]
 
-    def forward_head(h):
-        drain(xin.at[h], in_sem.at[h])
-
-        def body(r, carry):
-            forward_row(h, r)
-            return carry
-
-        lax.fori_loop(0, rows, body, 0)
-
-    def send_stats():
+    def send_stats(h):
+        pair = pl.ds(2 * h, 2)
         for d in range(1, m):
             peer = (p + d) % m
-            send(st_row.at[:, peer], st_own.at[:, p], s_send, s_recv, first + peer)
-        st_own[:, p] = st_row[:, p]
-
-        @pl.when(outer)
-        def _():
-            drain(st_own.at[:, pl.ds(0, m - 1)], s_recv)
-            send(st_own, st_far, sf_send, sf_recv, inner_peer)
-
-    def wait_stats():
-        drain(st_own.at[:, pl.ds(0, m - 1)], s_recv)
-        drain(st_far, sf_recv)
+            send(st_row.at[pair, peer], st_own.at[pair, p], s_send, s_recv.at[h], first + peer)
+        st_own[pair, p] = st_row[pair, p]
+
+    def wait_stats(h):
+        drain(st_own.at[pl.ds(2 * h, 2), pl.ds(0, m - 1)], s_recv.at[h])
+
+    def pass_stats(h):
+        wait_stats(h)
+        pair = pl.ds(2 * h, 2)
+        send(st_own.at[pair], st_far.at[pair], sf_send, sf_recv.at[h], inner_peer)
 
     def tile(ref, *at):
         return ref[at].reshape(plane_rows * GROUP, HEAD_DIM)
@@ -523,6 +514,8 @@
 
         @pl.when(part == 0)
         def _():
+            wait_stats(h)
+            drain(st_far.at[pl.ds(2 * h, 2)], sf_recv.at[h])
             lse_own[h] = jnp.zeros(lse_own.shape[1:], F32)
             lse_far[h] = jnp.zeros(lse_far.shape[1:], F32)
 
@@ -672,35 +665,64 @@
             give(2, j, gk[j] * SCALE + came_back(2, j))
             give(3, j, gv[j] + came_back(3, j))
 
-    def backward_head(h):
+    def backward_ready(h):
         drain(back.at[h, :, :, pl.ds(0, blocks * (m - 1))], e_recv.at[h])
         drain(lse_back.at[h, pl.ds(0, m - 1)], le_recv.at[h])
 
-        def body(r, carry):
-            backward_row(h, r)
-            return carry
-
-        lax.fori_loop(0, rows, body, 0)
+    def give_out(h):
         for kind in range(4):
             pltpu.make_async_copy(
                 back.at[h, kind], outs[kind].at[:, :, :, lanes_of(h)], out_sem
             ).start()
 
     lag_upper, lag_lower, lag_edge, lag_rows = LAGS
+    pace = splits // rows
+
+    def rows_forward(s):
+        h = s // splits + 1
+
+        @pl.when((h < heads) & (s % splits == 0))
+        def _():
+            drain(xin.at[h], in_sem.at[h])
+
+        @pl.when((h < heads) & (s % pace == 0))
+        def _():
+            forward_row(h, s % splits // pace)
+
+        @pl.when((h < heads) & (s % splits == (rows - 1) * pace))
+        def _():
+            send_stats(h)
+
+        @pl.when((h < heads) & (s % splits == splits - 1) & outer)
+        def _():
+            pass_stats(h)
+
+    def rows_backward(t):
+        h = t // splits
+        last = h == heads - 1
+
+        @pl.when((t >= 0) & (t % splits == 0))
+        def _():
+            backward_ready(h)
+
+        @pl.when((t >= 0) & (t % pace == 0))
+        def _():
+            def body(r, carry):
+                backward_row(h, r)
+                return carry
+
+            start = jnp.where(last, 0, t % splits // pace)
+            lax.fori_loop(start, jnp.where(last, rows, start + 1), body, 0)
+
+        @pl.when((t >= 0) & (last | (t % splits == (rows - 1) * pace)))
+        def _():
+            give_out(h)
 
     def step(s, carry):
         def at(lag, role=None):
             ready = (s >= lag) & (s < chunks + lag)
             return ready if role is None else ready & role
 
-        @pl.when(s < heads)
-        def _():
-            forward_head(s)
-
-        @pl.when(s == heads - 1)
-        def _():
-            send_stats()
-
         @pl.when(at(0))
         def _():
             pass_on(s)
@@ -713,9 +735,9 @@
         def _():
             pass_far(s - 1)
 
-        @pl.when((s == lag_upper) & ((z == 1) | (z == 2)))
-        def _():
-            wait_stats()
+        @pl.when((s == 0) & outer)
+        def _():
+            pass_stats(0)
 
         @pl.when(at(lag_upper, z == 2))
         def _():
@@ -729,14 +751,18 @@
         def _():
             edge(s - lag_edge)
 
-        done = s - lag_rows
-
-        @pl.when((done >= 0) & (done % splits == splits - 1))
-        def _():
-            backward_head(done // splits)
-
+        rows_forward(s)
+        rows_backward(s - lag_rows - (splits - 1))
         return carry
 
+    drain(xin.at[0], in_sem.at[0])
+
+    def first_head(r, carry):
+        forward_row(0, r)
+        return carry
+
+    lax.fori_loop(0, rows, first_head, 0)
+    send_stats(0)
     lax.fori_loop(0, chunks + lag_rows, step, 0)
 
     drain(own.at[:, :, pl.ds(0, rows * (m - 1))], a_send)
@@ -762,7 +788,7 @@
 
 
 AHEAD = 2
-LAGS = (3, 6, 8, 11)
+LAGS = (2, 5, 7, 9)
 
 
 def fits(tokens, width, devices):
@@ -776,6 +802,7 @@
         and ROW_LEN // m == LANES
         and rows * m * GROUP == LANES
         and (blocks // m) % SPLITS == 0
+        and SPLITS % rows == 0
     )
 
 
@@ -807,8 +834,8 @@
             stat, stat, stat, lse, lse, lse,
             dma((heads,)), each, single, each, single, each, dma((chunks, 2)),
             each, each, each, each, single, each, single, each,
-            single, dma((heads,)), single, single, single, single, single, dma((heads,)),
-            single, dma((heads,)), single,
+            single, dma((heads,)), single, dma((heads,)), single, dma((heads,)),
+            single, dma((heads,)), single, dma((heads,)), single,
         ],
         compiler_params=pltpu.CompilerParams(
             collective_id=0, has_side_effects=True, vmem_limit_bytes=63 * 1024 * 1024

time: 244 us -> 235 us (0.963)
  Pallas kernels: 234 us -> 224 us
    pallas_call x1, Pallas kernels: 234 us -> 224 us  [by_planes(): pl.pallas_call(fused_kernel, in_specs=[pl.BlockSpec(memory_space=pl.ANY)]...]
where the time goes in v3:
time: 235 us; the launch traced here: 234 us
  Pallas kernels  224 us (95%)
  local copies, waits for them, and re-layouts  9.21 us (4%)
    pallas_call x1, Pallas kernels, by_planes(): pl.pallas_call(fused_kernel, in_specs=[pl.BlockSpec(memory_space=pl.ANY)]...  224 us
    unnamed x10, local copies, waits for them, and re-layouts  9.21 us

profile of v3, /device:TPU:0, one launch (start us, length us, event | category | flops | bytes accessed | tf_op | source)
XLA Modules:
  0.0 234.4 jit_solution(14866418675300672302)
XLA Ops:
  0.6 224.5 %by_planes.1 = (bf16[4,64,8,512]{3,2,1,0:T(8,128)(2,1)}, bf16[4,64,8,512]{3,2,1,0:T(8,128)(2,1)}, bf16[4,64,8,512]{3,2,1,0:T(8,128)(2,1)}, bf16[4,64,8,512]{3,2,1,0:T(8,128)(2,1)}) custom-call(bf16[4,64,8,512]{3,2,1,0:T(8,128)(2,1)} %bitcast.16, bf16[4,64,8,512]{3,2,1,0:T(8,128)(2,1)} %bitcast.18, bf16[4,64,8,512]{3,2,1,0:T(8,128)(2,1)} %bitcast.20, ...), custom_call_target="tpu_custom_call" | custom-call | flops 12884901888 | bytes 16777216 | tf_op jit(solution)/shard_map/by_planes/pallas_call | solution.py:824
  225.1 0.0 copy-start.2
  225.1 3.2 %copy.12 = bf16[2048,512]{1,0:T(8,128)(2,1)} copy(bf16[2048,512]{1,0:T(8,128)(2,1)} %bitcast.15) | data formatting | bytes 4194304
  228.3 0.0 copy-done.2
  228.3 0.0 copy-start.1
  228.3 1.3 copy.13
  229.7 1.0 copy-done.1
  230.7 0.0 copy-start
  230.7 1.3 copy.14
  232.0 1.0 copy-done
  233.0 1.3 copy.15
Async XLA Ops:
  225.1 3.2 %copy-start.2 = (bf16[4,64,8,512]{3,2,1,0:T(8,128)(2,1)S(1)}, bf16[4,64,8,512]{3,2,1,0:T(8,128)(2,1)}, u32[]{:S(2)}) copy-start(bf16[4,64,8,512]{3,2,1,0:T(8,128)(2,1)} %get-tuple-element.9) | copy-start | bytes 6291460
  228.3 2.3 %copy-start.1 = (bf16[4,64,8,512]{3,2,1,0:T(8,128)(2,1)S(1)}, bf16[4,64,8,512]{3,2,1,0:T(8,128)(2,1)}, u32[]{:S(2)}) copy-start(bf16[4,64,8,512]{3,2,1,0:T(8,128)(2,1)} %get-tuple-element.10) | copy-start | bytes 6291460
  230.7 2.3 %copy-start = (bf16[4,64,8,512]{3,2,1,0:T(8,128)(2,1)S(1)}, bf16[4,64,8,512]{3,2,1,0:T(8,128)(2,1)}, u32[]{:S(2)}) copy-start(bf16[4,64,8,512]{3,2,1,0:T(8,128)(2,1)} %get-tuple-element.11) | copy-start | bytes 6291460

commit v4 on v3

--- a/solution.py
+++ b/solution.py
@@ -391,13 +391,86 @@
     return out_low, (gq * SCALE).T.astype(BF16), gk, gv, lse_col
 
 
+def stat_line(ref, r, i):
+    base = i * (CHUNK // LANES)
+    return jnp.concatenate(
+        [ref[base + n, pl.ds(r, 1), :] for n in range(CHUNK // LANES)], axis=1
+    )
+
+
+def row_gradients(q, k, v, g, o_row, lse_row, lse_col, came_back, give):
+    count = q.shape[0] // CHUNK
+    gk, gv = [None] * count, [None] * count
+    for i in range(count):
+        span = slice(i * CHUNK, (i + 1) * CHUNK)
+        lse, w_row, w_col = merge(lse_row(i), lse_col(i))
+        att_t = o_row(span) * w_row + came_back(0, i).T * w_col
+        att = att_t.T.astype(BF16)
+        give(0, i, att)
+        delta = jnp.sum(
+            (chunk(g, i).astype(F32) * att.astype(F32)).T, axis=0, keepdims=True
+        )
+        scores = scores_of(chunk(q, i), k, row_bias, i)
+        probs = [jnp.exp2(s - lse) for s in scores]
+        gq = backward_of(i, probs, delta, q, k, v, g, gk, gv)
+        give(1, i, gq + came_back(1, i))
+    for j in range(count):
+        give(2, j, gk[j] * SCALE + came_back(2, j))
+        give(3, j, gv[j] + came_back(3, j))
+
+
+def tail_kernel(*refs):
+    done, (q, k, v, g) = refs[0:4], [ref[0] for ref in refs[4:8]]
+    back, o_row, st_row, lse_back = refs[8:12]
+    outs = refs[12:]
+    r = pl.program_id(0)
+    width = done[0].shape[2]
+
+    def came_back(kind, i):
+        return back[kind, 0, i * CHUNK:(i + 1) * CHUNK].astype(F32)
+
+    def give(kind, i, value):
+        outs[kind][0, i * CHUNK:(i + 1) * CHUNK, width:] = value.astype(BF16)
+
+    for n in range(4):
+        outs[n][0, :, :width] = done[n][0]
+    row_gradients(
+        q, k, v, g,
+        lambda span: o_row[0, :, span],
+        lambda i: stat_line(st_row, r, i),
+        lambda i: stat_line(lse_back, r, i),
+        came_back, give,
+    )
+
+
+def finish(done, flat, back, o_row, st_row, lse_back):
+    rows, length, width = flat[0].shape
+    last = width // HEAD_DIM - 1
+    lines = pl.BlockSpec(st_row.shape, lambda r: (0, 0, 0))
+    return pl.pallas_call(
+        tail_kernel,
+        grid=(rows,),
+        in_specs=[pl.BlockSpec((1, length, done[0].shape[2]), lambda r: (r, 0, 0))] * 4
+        + [pl.BlockSpec((1, length, HEAD_DIM), lambda r: (r, 0, last))] * 4
+        + [
+            pl.BlockSpec((4, 1, length, HEAD_DIM), lambda r: (0, r, 0, 0)),
+            pl.BlockSpec((1, HEAD_DIM, length), lambda r: (r, 0, 0)),
+            lines, lines,
+        ],
+        out_specs=[pl.BlockSpec((1, length, width), lambda r: (r, 0, 0))] * 4,
+        out_shape=[jax.ShapeDtypeStruct((rows, length, width), BF16)] * 4,
+        name="finish",
+    )(*done, *flat, back, o_row, st_row, lse_back)
+
+
 def fused_kernel(*refs):
     xs, flat, outs = refs[0:4], refs[4:8], refs[8:12]
+    tail_back, tail_o, tail_row, tail_col = refs[12:16]
     (xin, own, far, low, back, orow, st_row, st_own, st_far, lse_own, lse_far,
      lse_back, in_sem, a_loc, a_send, a_recv, b_send, bkv_recv, bqg_recv,
      k1_send, k1_recv, k0_send, k0_recv, d2_send, d2_recv, d1_send, d1_recv,
      e_send, e_recv, s_send, s_recv, sf_send, sf_recv, l1_send, l1_recv,
-     le_send, le_recv, out_sem) = refs[12:]
+     le_send, le_recv, out_sem, tail_sem) = refs[16:]
     heads, _, rows = xin.shape[:3]
     chunks = own.shape[0]
     plane_rows, per = own.shape[2], own.shape[3]
@@ -632,8 +705,6 @@
         return_rows(c, far)
 
     def backward_row(h, r):
-        q, k, v, g = [xin[h, kind, r] for kind in range(4)]
-        count = q.shape[0] // CHUNK
         slab = CHUNK // GROUP
 
         def came_back(kind, i):
@@ -642,28 +713,13 @@
         def give(kind, i, value):
             back[h, kind, r, i * slab:(i + 1) * slab] = value.astype(BF16).reshape(slab, GROUP, HEAD_DIM)
 
-        def line(ref, lead, i):
-            base = i * (CHUNK // LANES)
-            return jnp.concatenate(
-                [ref[lead, base + n, pl.ds(r, 1), :] for n in range(CHUNK // LANES)], axis=1)
-
-        gk, gv = [None] * count, [None] * count
-        for i in range(count):
-            span = slice(i * CHUNK, (i + 1) * CHUNK)
-            lse, w_row, w_col = merge(line(st_row, 2 * h, i), line(lse_back, h, i))
-            att_t = orow[h, r, :, span] * w_row + came_back(0, i).T * w_col
-            att = att_t.T.astype(BF16)
-            give(0, i, att)
-            delta = jnp.sum(
-                (chunk(g, i).astype(F32) * att.astype(F32)).T, axis=0, keepdims=True
-            )
-            scores = scores_of(chunk(q, i), k, row_bias, i)
-            probs = [jnp.exp2(s - lse) for s in scores]
-            gq = backward_of(i, probs, delta, q, k, v, g, gk, gv)
-            give(1, i, gq + came_back(1, i))
-        for j in range(count):
-            give(2, j, gk[j] * SCALE + came_back(2, j))
-            give(3, j, gv[j] + came_back(3, j))
+        row_gradients(
+            *[xin[h, kind, r] for kind in range(4)],
+            lambda span: orow[h, r, :, span],
+            lambda i: stat_line(st_row.at[2 * h], r, i),
+            lambda i: stat_line(lse_back.at[h], r, i),
+            came_back, give,
+        )
 
     def backward_ready(h):
         drain(back.at[h, :, :, pl.ds(0, blocks * (m - 1))], e_recv.at[h])
@@ -697,24 +753,23 @@
         def _():
             pass_stats(h)
 
+        @pl.when((h == heads - 1) & (s % splits == splits - 1))
+        def _():
+            pltpu.make_async_copy(orow.at[h], tail_o, tail_sem.at[2]).start()
+            pltpu.make_async_copy(st_row.at[2 * h], tail_row, tail_sem.at[3]).start()
+
     def rows_backward(t):
         h = t // splits
-        last = h == heads - 1
 
         @pl.when((t >= 0) & (t % splits == 0))
         def _():
             backward_ready(h)
 
-        @pl.when((t >= 0) & (t % pace == 0))
-        def _():
-            def body(r, carry):
-                backward_row(h, r)
-                return carry
-
-            start = jnp.where(last, 0, t % splits // pace)
-            lax.fori_loop(start, jnp.where(last, rows, start + 1), body, 0)
-
-        @pl.when((t >= 0) & (last | (t % splits == (rows - 1) * pace)))
+        @pl.when((t >= 0) & (h < heads - 1) & (t % pace == 0))
+        def _():
+            backward_row(h, t % splits // pace)
+
+        @pl.when((t >= 0) & (h < heads - 1) & (t % splits == (rows - 1) * pace))
         def _():
             give_out(h)
 
@@ -784,7 +839,18 @@
     def _():
         drain(low, d2_send)
 
-    drain(back, out_sem)
+    last = heads - 1
+    copies = [
+        pltpu.make_async_copy(back.at[last], tail_back, tail_sem.at[0]),
+        pltpu.make_async_copy(lse_back.at[last], tail_col, tail_sem.at[1]),
+    ]
+    for copy in copies:
+        copy.start()
+    for copy in copies:
+        copy.wait()
+    pltpu.make_async_copy(orow.at[last], tail_o, tail_sem.at[2]).wait()
+    pltpu.make_async_copy(st_row.at[2 * last], tail_row, tail_sem.at[3]).wait()
+    drain(back.at[pl.ds(0, last)], out_sem)
 
 
 AHEAD = 2
@@ -799,6 +865,7 @@
     blocks = ROW_LEN // GROUP
     return (
         m > 1
+        and width > HEAD_DIM
         and ROW_LEN // m == LANES
         and rows * m * GROUP == LANES
         and (blocks // m) % SPLITS == 0
@@ -824,8 +891,14 @@
     outs = pl.pallas_call(
         fused_kernel,
         in_specs=[pl.BlockSpec(memory_space=pl.ANY)] * 8,
-        out_specs=[pl.BlockSpec(memory_space=pl.ANY)] * 4,
-        out_shape=[jax.ShapeDtypeStruct(views[0].shape, BF16)] * 4,
+        out_specs=[pl.BlockSpec(memory_space=pl.ANY)] * 8,
+        out_shape=[jax.ShapeDtypeStruct((rows, blocks, GROUP, width - HEAD_DIM), BF16)] * 4
+        + [
+            jax.ShapeDtypeStruct((4, rows, blocks, GROUP, HEAD_DIM), BF16),
+            jax.ShapeDtypeStruct((rows, HEAD_DIM, ROW_LEN), F32),
+            jax.ShapeDtypeStruct((m, rows, LANES), F32),
+            jax.ShapeDtypeStruct((m, rows, LANES), F32),
+        ],
         scratch_shapes=[
             pltpu.VMEM((heads, 4, rows, ROW_LEN, HEAD_DIM), BF16),
             buffer, buffer, buffer,
@@ -835,7 +908,7 @@
             dma((heads,)), each, single, each, single, each, dma((chunks, 2)),
             each, each, each, each, single, each, single, each,
             single, dma((heads,)), single, dma((heads,)), single, dma((heads,)),
-            single, dma((heads,)), single, dma((heads,)), single,
+            single, dma((heads,)), single, dma((heads,)), single, dma((4,)),
         ],
         compiler_params=pltpu.CompilerParams(
             collective_id=0, has_side_effects=True, vmem_limit_bytes=63 * 1024 * 1024
@@ -847,6 +920,9 @@
         ),
         name="by_planes",
     )(*views, *flat)
+    done = [a.reshape(rows, ROW_LEN, width - HEAD_DIM) for a in outs[:4]]
+    back = outs[4].reshape(4, rows, ROW_LEN, HEAD_DIM)
+    outs = finish(done, flat, back, *outs[5:])
     return tuple(a.reshape(queries.shape) for a in outs)
 
 

time: 235 us -> 231 us (0.983)
  local copies, waits for them, and re-layouts: 9.21 us -> 0 us
  Pallas kernels: 224 us -> 230 us
    pallas_call x0 -> x1, Pallas kernels: none -> 9.85 us  [finish(): pl.pallas_call(tail_kernel, grid=(rows,), in_specs=[pl.BlockSpec((1, leng...]
    unnamed x10 -> x0, local copies, waits for them, and re-layouts: 9.21 us -> none
    pallas_call x1, Pallas kernels: 224 us -> 220 us  [by_planes(): pl.pallas_call(fused_kernel, in_specs=[pl.BlockSpec(memory_space=pl.ANY)]...]
where the time goes in v4:
time: 231 us
  Pallas kernels  230 us (100%)
    pallas_call x1, Pallas kernels, by_planes(): pl.pallas_call(fused_kernel, in_specs=[pl.BlockSpec(memory_space=pl.ANY)]...  220 us
    pallas_call x1, Pallas kernels, finish(): pl.pallas_call(tail_kernel, grid=(rows,), in_specs=[pl.BlockSpec((1, leng...  9.85 us

profile of v4, /device:TPU:0, one launch (start us, length us, event | category | flops | bytes accessed | tf_op | source)
XLA Modules:
  0.0 230.6 jit_solution(17849515660714039461)
XLA Ops:
  0.6 220.1 %by_planes.1 = (bf16[4,64,8,384]{3,2,1,0:T(8,128)(2,1)}, bf16[4,64,8,384]{3,2,1,0:T(8,128)(2,1)}, bf16[4,64,8,384]{3,2,1,0:T(8,128)(2,1)}, bf16[4,64,8,384]{3,2,...) custom-call(bf16[4,64,8,512]{3,2,1,0:T(8,128)(2,1)} %bitcast.17, ...), custom_call_target="tpu_custom_call" | custom-call | flops 12884901888 | bytes 16777216 | tf_op jit(solution)/shard_map/by_planes/pallas_call | solution.py:891
  220.7 9.9 %finish.1 = (bf16[4,512,512]{2,1,0:T(8,128)(2,1)}, bf16[4,512,512]{2,1,0:T(8,128)(2,1)}, bf16[4,512,512]{2,1,0:T(8,128)(2,1)}, bf16[4,512,512]{2,1,0:T(8,128)(2,1)}) custom-call(bf16[4,512,384]{2,1,0:T(8,128)(2,1)} %bitcast.30, bf16[4,512,384]{2,1,0:T(8,128)(2,1)} %bitcast.31, bf16[4,512,384]{2,1,0:T(8,128)(2,1)} %bitcast.32, bf16[4,512,384]{2,1,0:T(8,128)(2,1)} %bitcast.33, ...), custom_call_target="tpu_custom_call" | custom-call | tf_op jit(solution)/shard_map/finish/pallas_call | solution.py:450

commit v5 on v3

--- a/solution.py
+++ b/solution.py
@@ -391,12 +391,72 @@
     return out_low, (gq * SCALE).T.astype(BF16), gk, gv, lse_col
 
 
+def stat_line(ref, r, i):
+    base = i * (CHUNK // LANES)
+    return jnp.concatenate(
+        [ref[base + n, pl.ds(r, 1), :] for n in range(CHUNK // LANES)], axis=1
+    )
+
+
+def row_gradients(q, k, v, g, o_row, lse_row, lse_col, came_back, give):
+    count = q.shape[0] // CHUNK
+    gk, gv = [None] * count, [None] * count
+    for i in range(count):
+        span = slice(i * CHUNK, (i + 1) * CHUNK)
+        lse, w_row, w_col = merge(lse_row(i), lse_col(i))
+        att_t = o_row(span) * w_row + came_back(0, i).T * w_col
+        att = att_t.T.astype(BF16)
+        give(0, i, att)
+        delta = jnp.sum(
+            (chunk(g, i).astype(F32) * att.astype(F32)).T, axis=0, keepdims=True
+        )
+        scores = scores_of(chunk(q, i), k, row_bias, i)
+        probs = [jnp.exp2(s - lse) for s in scores]
+        gq = backward_of(i, probs, delta, q, k, v, g, gk, gv)
+        give(1, i, gq + came_back(1, i))
+    return gk, gv
+
+
+def copy_kernel(*refs):
+    ins, outs = refs[0:4], refs[4:8]
+    held, in_sem, out_sem = refs[8:]
+    rows = held.shape[1]
+    fetches = [
+        pltpu.make_async_copy(ins[n].at[r], held.at[n, r], in_sem.at[n, r])
+        for r in range(rows) for n in range(4)
+    ]
+    stores = [
+        pltpu.make_async_copy(held.at[n, r], outs[n].at[r], out_sem.at[n, r])
+        for r in range(rows) for n in range(4)
+    ]
+    for fetch in fetches:
+        fetch.start()
+    for fetch, store in zip(fetches, stores):
+        fetch.wait()
+        store.start()
+    for store in stores:
+        store.wait()
+
+
+def copy_out(arrays):
+    shape = arrays[0].shape
+    sems = pltpu.SemaphoreType.DMA((4, shape[0]))
+    return pl.pallas_call(
+        copy_kernel,
+        in_specs=[pl.BlockSpec(memory_space=pl.ANY)] * 4,
+        out_specs=[pl.BlockSpec(memory_space=pl.ANY)] * 4,
+        out_shape=[jax.ShapeDtypeStruct(shape, BF16)] * 4,
+        scratch_shapes=[pltpu.VMEM((4, *shape), BF16), sems, sems],
+        name="copy_out",
+    )(*arrays)
+
+
 def fused_kernel(*refs):
     xs, flat, outs = refs[0:4], refs[4:8], refs[8:12]
-    (xin, own, far, low, back, orow, st_row, st_own, st_far, lse_own, lse_far,
-     lse_back, in_sem, a_loc, a_send, a_recv, b_send, bkv_recv, bqg_recv,
-     k1_send, k1_recv, k0_send, k0_recv, d2_send, d2_recv, d1_send, d1_recv,
-     e_send, e_recv, s_send, s_recv, sf_send, sf_recv, l1_send, l1_recv,
+    (xin, own, far, low, back, orow, ring, row_sum, st_row, st_own, st_far,
+     lse_own, lse_far, lse_back, in_sem, a_loc, a_send, a_recv, b_send, bkv_recv,
+     bqg_recv, k1_send, k1_recv, k0_send, k0_recv, d2_send, d2_recv, d1_send,
+     d1_recv, f1_send, f1_recv, e_send, e_recv, g_send, g_recv, s_send, s_recv, sf_send, sf_recv, l1_send, l1_recv,
      le_send, le_recv, out_sem) = refs[12:]
     heads, _, rows = xin.shape[:3]
     chunks = own.shape[0]
@@ -463,7 +523,7 @@
     lax.fori_loop(1, heads, load_rows, 0)
 
     def forward_row(h, r):
-        q, k, v, g = [xin[h, kind, r] for kind in range(4)]
+        q, g, k, v = [xin[h, kind, r] for kind in range(4)]
         for i in range(q.shape[0] // CHUNK):
             span = slice(i * CHUNK, (i + 1) * CHUNK)
             _, top, total, out = softmax_of(scores_of(chunk(q, i), k, row_bias, i), v)
@@ -526,7 +586,7 @@
             def both(kind):
                 return jnp.concatenate([tile(ref, c, kind, every, b) for ref in pair], axis=0)
 
-            q, k, v, g = [both(kind) for kind in range(4)]
+            q, g, k, v = [both(kind) for kind in range(4)]
             keys, values = [k], [v]
             if not lower:
                 keys = [jnp.concatenate([tile(low, c, 0, every, b), tile(low, c, 2, every, b)], axis=0), k]
@@ -534,36 +594,52 @@
             lse_row = jnp.concatenate([stat_of(s, 2 * h, block) for s in stats], axis=1)
             dot_row = jnp.concatenate([stat_of(s, 2 * h + 1, block) for s in stats], axis=1)
             o, gq, gk, gv, lse_col = column_unit(q, g, keys, values, None, lse_row, dot_row)
-            gk_own, gv_own = gk[-1], gv[-1]
             if lower:
-                gk_own = gk_own + jnp.concatenate(
-                    [tile(low, c, 0, every, b), tile(low, c, 2, every, b)], axis=0).astype(F32)
-                gv_own = gv_own + jnp.concatenate(
-                    [tile(low, c, 1, every, b), tile(low, c, 3, every, b)], axis=0).astype(F32)
+                ring[c % ring.shape[0], b, 0] = gk[-1]
+                ring[c % ring.shape[0], b, 1] = gv[-1]
+                values = (o, gq)
             else:
                 put(low, (c, 0, every, b), gk[0][:half])
                 put(low, (c, 1, every, b), gv[0][:half])
                 put(low, (c, 2, every, b), gk[0][half:])
                 put(low, (c, 3, every, b), gv[0][half:])
+                values = (o, gq, gk[-1], gv[-1])
             for n, ref in enumerate(pair):
                 span = slice(n * half, (n + 1) * half)
-                for kind, value in enumerate((o, gq, gk_own, gv_own)):
+                for kind, value in enumerate(values):
                     put(ref, (c, kind, every, b), value[span])
                 add_lse(lses[n], h, lse_col[:, span], block)
             return carry
 
         lax.fori_loop(0, per, body, 0)
 
-    def return_rows(c, ref):
+    def add_upper(c):
+        def body(b, carry):
+            for kind in range(2):
+                total = ring[c % ring.shape[0], b, kind]
+                for n, ref in enumerate((far, own)):
+                    share = tile(low, c, 2 * n + kind, slice(None), b).astype(F32)
+                    put(ref, (c, 2 + kind, slice(None), b), total[n * half:(n + 1) * half] + share)
+            return carry
+
+        lax.fori_loop(0, per, body, 0)
+
+    early, late = pl.ds(0, 2), pl.ds(2, 2)
+
+    def return_rows(c, ref, kinds, send_sem, recv_sem):
         h, part = c // splits, c % splits
         at = pl.ds(p * blocks + part * per, per)
         for d in range(1, m):
             peer = (p + d) % m
             send(
-                ref.at[c, :, pl.ds(peer * rows, rows)], back.at[h, :, :, at],
-                e_send, e_recv.at[h], first + peer,
+                ref.at[c, kinds, pl.ds(peer * rows, rows)], back.at[h, kinds, :, at],
+                send_sem, recv_sem.at[h], first + peer,
             )
-        back[h, :, :, at] = ref[c, :, pl.ds(p * rows, rows)]
+        back[h, kinds, :, at] = ref[c, kinds, pl.ds(p * rows, rows)]
+
+    def return_first(c, ref):
+        h, part = c // splits, c % splits
+        return_rows(c, ref, early, e_send, e_recv)
 
         @pl.when(part == splits - 1)
         def _():
@@ -572,13 +648,19 @@
                 send(lse_own.at[h, peer], lse_back.at[h, p], le_send, le_recv.at[h], first + peer)
             lse_back[h, p] = lse_own[h, p]
 
-    def return_far(c):
+    def return_second(c, ref):
+        return_rows(c, ref, late, g_send, g_recv)
+
+    def far_first(c):
         h, part = c // splits, c % splits
-        send(far.at[c], far.at[c], d1_send, d1_recv.at[c], outer_peer)
+        send(far.at[c, early], far.at[c, early], d1_send, d1_recv.at[c], outer_peer)
 
         @pl.when(part == splits - 1)
         def _():
             send(lse_far.at[h], lse_own.at[h], l1_send, l1_recv.at[h], outer_peer)
+
+    def far_second(c):
+        send(far.at[c, late], far.at[c, late], f1_send, f1_recv.at[c], outer_peer)
 
     def pass_on(c):
         drain(own.at[c, :, pl.ds(0, rows * (m - 1))], a_recv.at[c])
@@ -586,54 +668,58 @@
 
         @pl.when(outer)
         def _():
-            send(own.at[c, pl.ds(1, 2)], far.at[c, pl.ds(1, 2)], b_send, bkv_recv.at[c], inner_peer)
-            send(own.at[c, 0], far.at[c, 0], b_send, bqg_recv.at[c, 0], inner_peer)
-            send(own.at[c, 3], far.at[c, 3], b_send, bqg_recv.at[c, 1], inner_peer)
+            send(own.at[c, late], far.at[c, late], b_send, bkv_recv.at[c], inner_peer)
+            send(own.at[c, early], far.at[c, early], b_send, bqg_recv.at[c], inner_peer)
 
         @pl.when(z == 1)
         def _():
-            send(own.at[c, pl.ds(1, 2)], low.at[c, pl.ds(2, 2)], k1_send.at[c], k1_recv.at[c], seq + m)
+            send(own.at[c, late], low.at[c, pl.ds(2, 2)], k1_send.at[c], k1_recv.at[c], seq + m)
 
     def pass_far(c):
-        drain(far.at[c, pl.ds(1, 2)], bkv_recv.at[c])
-        send(far.at[c, pl.ds(1, 2)], low.at[c, pl.ds(0, 2)], k0_send.at[c], k0_recv.at[c], seq + m)
-
-    def wait_qg(c):
-        drain(far.at[c, 0], bqg_recv.at[c, 0])
-        drain(far.at[c, 3], bqg_recv.at[c, 1])
+        drain(far.at[c, late], bkv_recv.at[c])
+        send(far.at[c, late], low.at[c, pl.ds(0, 2)], k0_send.at[c], k0_recv.at[c], seq + m)
 
     def upper(c):
-        drain(far.at[c, pl.ds(1, 2)], bkv_recv.at[c])
-        wait_qg(c)
+        drain(far.at[c, late], bkv_recv.at[c])
+        drain(far.at[c, early], bqg_recv.at[c])
         drain(low.at[c, pl.ds(2, 2)], k1_recv.at[c])
         drain(low.at[c, pl.ds(0, 2)], k0_recv.at[c])
         solve(c, False)
         send(low.at[c], low.at[c], d2_send, d2_recv.at[c], seq - m)
-        return_far(c)
-        return_rows(c, own)
-
-    def lower(c):
-        wait_qg(c)
+        far_first(c)
+        return_first(c, own)
+        far_second(c)
+        return_second(c, own)
+
+    def lower_first(c):
+        drain(far.at[c, early], bqg_recv.at[c])
+        solve(c, True)
+        far_first(c)
+        return_first(c, own)
+
+    def lower_second(c):
         drain(low.at[c], d2_recv.at[c])
-        drain(own.at[c, pl.ds(1, 2)], k1_send.at[c])
-        drain(far.at[c, pl.ds(1, 2)], k0_send.at[c])
-        solve(c, True)
-        return_far(c)
-        return_rows(c, own)
-
-    def edge(c):
+        drain(own.at[c, late], k1_send.at[c])
+        drain(far.at[c, late], k0_send.at[c])
+        add_upper(c)
+        far_second(c)
+        return_second(c, own)
+
+    def edge_first(c):
         h, part = c // splits, c % splits
-        drain(far.at[c], d1_recv.at[c])
+        drain(far.at[c, early], d1_recv.at[c])
 
         @pl.when(part == splits - 1)
         def _():
             drain(lse_own.at[h], l1_recv.at[h])
 
-        return_rows(c, far)
+        return_first(c, far)
+
+    def edge_second(c):
+        drain(far.at[c, late], f1_recv.at[c])
+        return_second(c, far)
 
     def backward_row(h, r):
-        q, k, v, g = [xin[h, kind, r] for kind in range(4)]
-        count = q.shape[0] // CHUNK
         slab = CHUNK // GROUP
 
         def came_back(kind, i):
@@ -642,40 +728,45 @@
         def give(kind, i, value):
             back[h, kind, r, i * slab:(i + 1) * slab] = value.astype(BF16).reshape(slab, GROUP, HEAD_DIM)
 
-        def line(ref, lead, i):
-            base = i * (CHUNK // LANES)
-            return jnp.concatenate(
-                [ref[lead, base + n, pl.ds(r, 1), :] for n in range(CHUNK // LANES)], axis=1)
-
-        gk, gv = [None] * count, [None] * count
-        for i in range(count):
-            span = slice(i * CHUNK, (i + 1) * CHUNK)
-            lse, w_row, w_col = merge(line(st_row, 2 * h, i), line(lse_back, h, i))
-            att_t = orow[h, r, :, span] * w_row + came_back(0, i).T * w_col
-            att = att_t.T.astype(BF16)
-            give(0, i, att)
-            delta = jnp.sum(
-                (chunk(g, i).astype(F32) * att.astype(F32)).T, axis=0, keepdims=True
-            )
-            scores = scores_of(chunk(q, i), k, row_bias, i)
-            probs = [jnp.exp2(s - lse) for s in scores]
-            gq = backward_of(i, probs, delta, q, k, v, g, gk, gv)
-            give(1, i, gq + came_back(1, i))
-        for j in range(count):
-            give(2, j, gk[j] * SCALE + came_back(2, j))
-            give(3, j, gv[j] + came_back(3, j))
+        q, g, k, v = [xin[h, kind, r] for kind in range(4)]
+        gk, gv = row_gradients(
+            q, k, v, g,
+            lambda span: orow[h, r, :, span],
+            lambda i: stat_line(st_row.at[2 * h], r, i),
+            lambda i: stat_line(lse_back.at[h], r, i),
+            came_back, give,
+        )
+        for j in range(len(gk)):
+            span = slice(j * CHUNK, (j + 1) * CHUNK)
+            row_sum[r, 0, span] = gk[j] * SCALE
+            row_sum[r, 1, span] = gv[j]
+
+    ready = pl.ds(0, blocks * (m - 1))
 
     def backward_ready(h):
-        drain(back.at[h, :, :, pl.ds(0, blocks * (m - 1))], e_recv.at[h])
+        drain(back.at[h, early, :, ready], e_recv.at[h])
         drain(lse_back.at[h, pl.ds(0, m - 1)], le_recv.at[h])
 
-    def give_out(h):
-        for kind in range(4):
-            pltpu.make_async_copy(
-                back.at[h, kind], outs[kind].at[:, :, :, lanes_of(h)], out_sem
-            ).start()
-
-    lag_upper, lag_lower, lag_edge, lag_rows = LAGS
+    def give_out(h, kind):
+        pltpu.make_async_copy(
+            back.at[h, kind], outs[kind].at[:, :, :, lanes_of(h)], out_sem
+        ).start()
+
+    def backward_done(h):
+        drain(back.at[h, late, :, ready], g_recv.at[h])
+
+        def body(r, carry):
+            for n in range(2):
+                share = back[h, 2 + n, r].reshape(ROW_LEN, HEAD_DIM).astype(F32)
+                total = (row_sum[r, n] + share).astype(BF16)
+                back[h, 2 + n, r] = total.reshape(back.shape[3:])
+            return carry
+
+        lax.fori_loop(0, rows, body, 0)
+        give_out(h, 2)
+        give_out(h, 3)
+
+    lag_upper, lag_low1, lag_low2, lag_edge1, lag_edge2, lag_rows = LAGS
     pace = splits // rows
 
     def rows_forward(s):
@@ -705,7 +796,7 @@
         def _():
             backward_ready(h)
 
-        @pl.when((t >= 0) & (t % pace == 0))
+        @pl.when((t >= 0) & ((t % pace == 0) & ~last | (t == chunks - splits)))
         def _():
             def body(r, carry):
                 backward_row(h, r)
@@ -714,9 +805,14 @@
             start = jnp.where(last, 0, t % splits // pace)
             lax.fori_loop(start, jnp.where(last, rows, start + 1), body, 0)
 
-        @pl.when((t >= 0) & (last | (t % splits == (rows - 1) * pace)))
-        def _():
-            give_out(h)
+        @pl.when((t >= 0) & ((t % splits == splits - 1) & ~last | (t == chunks - splits)))
+        def _():
+            give_out(h, 0)
+            give_out(h, 1)
+
+        @pl.when((t >= 0) & (t % splits == splits - 1) & ~last)
+        def _():
+            backward_done(h)
 
     def step(s, carry):
         def at(lag, role=None):
@@ -743,13 +839,21 @@
         def _():
             upper(s - lag_upper)
 
-        @pl.when(at(lag_lower, z == 1))
-        def _():
-            lower(s - lag_lower)
-
-        @pl.when(at(lag_edge, outer))
-        def _():
-            edge(s - lag_edge)
+        @pl.when(at(lag_low1, z == 1))
+        def _():
+            lower_first(s - lag_low1)
+
+        @pl.when(at(lag_low2, z == 1))
+        def _():
+            lower_second(s - lag_low2)
+
+        @pl.when(at(lag_edge1, outer))
+        def _():
+            edge_first(s - lag_edge1)
+
+        @pl.when(at(lag_edge2, outer))
+        def _():
+            edge_second(s - lag_edge2)
 
         rows_forward(s)
         rows_backward(s - lag_rows - (splits - 1))
@@ -763,10 +867,12 @@
 
     lax.fori_loop(0, rows, first_head, 0)
     send_stats(0)
-    lax.fori_loop(0, chunks + lag_rows, step, 0)
+    lax.fori_loop(0, chunks + max(LAGS), step, 0)
+    backward_done(heads - 1)
 
     drain(own.at[:, :, pl.ds(0, rows * (m - 1))], a_send)
-    drain(own.at[:, :, pl.ds(0, rows * (m - 1))], e_send)
+    drain(own.at[:, early, pl.ds(0, rows * (m - 1))], e_send)
+    drain(own.at[:, late, pl.ds(0, rows * (m - 1))], g_send)
     drain(st_own.at[:, pl.ds(0, m - 1)], s_send)
     drain(lse_own.at[:, pl.ds(0, m - 1)], le_send)
 
@@ -777,7 +883,8 @@
 
     @pl.when((z == 1) | (z == 2))
     def _():
-        drain(far, d1_send)
+        drain(far.at[:, early], d1_send)
+        drain(far.at[:, late], f1_send)
         drain(lse_far, l1_send)
 
     @pl.when(z == 2)
@@ -788,7 +895,8 @@
 
 
 AHEAD = 2
-LAGS = (2, 5, 7, 9)
+RING = 8
+LAGS = (2, 2, 5, 4, 7, 6)
 
 
 def fits(tokens, width, devices):
@@ -813,14 +921,14 @@
     rows, heads, blocks = tokens // ROW_LEN, width // HEAD_DIM, ROW_LEN // GROUP
     per = blocks // m // SPLITS
     chunks = heads * SPLITS
-    arrays = (queries, key_vectors, value_vectors, grad_output)
+    arrays = (queries, grad_output, key_vectors, value_vectors)
     views = [a.reshape(rows, blocks, GROUP, width) for a in arrays]
     flat = [a.reshape(rows, ROW_LEN, width) for a in arrays]
     buffer = pltpu.VMEM((chunks, 4, rows * m, per, GROUP, HEAD_DIM), BF16)
     dma = pltpu.SemaphoreType.DMA
     stat = pltpu.VMEM((2 * heads, m, rows, LANES), F32)
     lse = pltpu.VMEM((heads, m, rows, LANES), F32)
-    each, single = dma((chunks,)), dma(())
+    each, by_head, single = dma((chunks,)), dma((heads,)), dma(())
     outs = pl.pallas_call(
         fused_kernel,
         in_specs=[pl.BlockSpec(memory_space=pl.ANY)] * 8,
@@ -831,11 +939,14 @@
             buffer, buffer, buffer,
             pltpu.VMEM((heads, 4, rows, blocks, GROUP, HEAD_DIM), BF16),
             pltpu.VMEM((heads, rows, HEAD_DIM, ROW_LEN), F32),
+            pltpu.VMEM((RING, per, 2, 2 * LANES, HEAD_DIM), F32),
+            pltpu.VMEM((rows, 2, ROW_LEN, HEAD_DIM), F32),
             stat, stat, stat, lse, lse, lse,
-            dma((heads,)), each, single, each, single, each, dma((chunks, 2)),
-            each, each, each, each, single, each, single, each,
-            single, dma((heads,)), single, dma((heads,)), single, dma((heads,)),
-            single, dma((heads,)), single, dma((heads,)), single,
+            by_head, each, single, each, single, each, each,
+            each, each, each, each, single, each, single,
+            each, single, each, single, by_head, single, by_head,
+            single, by_head, single, by_head, single, by_head, single, by_head,
+            single,
         ],
         compiler_params=pltpu.CompilerParams(
             collective_id=0, has_side_effects=True, vmem_limit_bytes=63 * 1024 * 1024
@@ -847,6 +958,7 @@
         ),
         name="by_planes",
     )(*views, *flat)
+    outs = copy_out(outs)
     return tuple(a.reshape(queries.shape) for a in outs)
 
 

time: 235 us -> 227 us (0.966)
  local copies, waits for them, and re-layouts: 9.21 us -> 0 us
    unnamed x10 -> x0, local copies, waits for them, and re-layouts: 9.21 us -> none
    pallas_call x0 -> x1, Pallas kernels: none -> 6.57 us  [copy_out(): pl.pallas_call(copy_kernel, in_specs=[pl.BlockSpec(memory_space=pl.ANY)]...]
    pallas_call x1, Pallas kernels: 224 us -> 219 us  [by_planes(): pl.pallas_call(fused_kernel, in_specs=[pl.BlockSpec(memory_space=pl.ANY)]...]
where the time goes in v5:
time: 227 us
  Pallas kernels  226 us (100%)
    pallas_call x1, Pallas kernels, by_planes(): pl.pallas_call(fused_kernel, in_specs=[pl.BlockSpec(memory_space=pl.ANY)]...  219 us
    pallas_call x1, Pallas kernels, copy_out(): pl.pallas_call(copy_kernel, in_specs=[pl.BlockSpec(memory_space=pl.ANY)]...  6.57 us

profile of v5, /device:TPU:0, one launch (start us, length us, event | category | flops | bytes accessed | tf_op | source)
XLA Modules:
  0.0 226.6 jit_solution(11335235629871509619)
XLA Ops:
  0.6 219.4 %by_planes.1 = (bf16[4,64,8,512]{3,2,1,0:T(8,128)(2,1)}, bf16[4,64,8,512]{3,2,1,0:T(8,128)(2,1)}, bf16[4,64,8,512]{3,2,1,0:T(8,128)(2,1)}, bf16[4,64,8,512]{3,2,1,0:T(8,128)(2,1)}) custom-call(bf16[4,64,8,512]{3,2,1,0:T(8,128)(2,1)} %bitcast.12, bf16[4,64,8,512]{3,2,1,0:T(8,128)(2,1)} %bitcast.14, bf16[4,64,8,512]{3,2,1,0:T(8,128)(2,1)} %bitcast.16, ...), custom_call_target="tpu_custom_call" | custom-call | flops 12884901888 | bytes 16777216 | tf_op jit(solution)/shard_map/by_planes/pallas_call | solution.py:932
  220.0 6.6 %copy_out.1 = (bf16[4,64,8,512]{3,2,1,0:T(8,128)(2,1)}, bf16[4,64,8,512]{3,2,1,0:T(8,128)(2,1)}, bf16[4,64,8,512]{3,2,1,0:T(8,128)(2,1)}, bf16[4,64,8,512]{3,2,1,0:T(8,128)(2,1)}) custom-call(bf16[4,64,8,512]{3,2,1,0:T(8,128)(2,1)} %get-tuple-element.12.refs_0_, bf16[4,64,8,512]{3,2,1,0:T(8,128)(2,1)} %get-tuple-element.13.refs_1_, ...), custom_call_target="tpu_custom_call" | custom-call | tf_op jit(solution)/shard_map/copy_out/pallas_call | solution.py:444

commit v6 on v5

--- a/solution.py
+++ b/solution.py
@@ -418,46 +418,38 @@
 
 
 def copy_kernel(*refs):
-    ins, outs = refs[0:4], refs[4:8]
-    held, in_sem, out_sem = refs[8:]
-    rows = held.shape[1]
-    fetches = [
-        pltpu.make_async_copy(ins[n].at[r], held.at[n, r], in_sem.at[n, r])
-        for r in range(rows) for n in range(4)
+    back, outs, sem = refs[0], refs[1:5], refs[5]
+    copies = [
+        pltpu.make_async_copy(
+            back.at[h, n], outs[n].at[:, :, :, h * HEAD_DIM:(h + 1) * HEAD_DIM], sem.at[h, n]
+        )
+        for h in range(back.shape[0]) for n in range(4)
     ]
-    stores = [
-        pltpu.make_async_copy(held.at[n, r], outs[n].at[r], out_sem.at[n, r])
-        for r in range(rows) for n in range(4)
-    ]
-    for fetch in fetches:
-        fetch.start()
-    for fetch, store in zip(fetches, stores):
-        fetch.wait()
-        store.start()
-    for store in stores:
-        store.wait()
-
-
-def copy_out(arrays):
-    shape = arrays[0].shape
-    sems = pltpu.SemaphoreType.DMA((4, shape[0]))
+    for copy in copies:
+        copy.start()
+    for copy in copies:
+        copy.wait()
+
+
+def copy_out(back, shape):
     return pl.pallas_call(
         copy_kernel,
-        in_specs=[pl.BlockSpec(memory_space=pl.ANY)] * 4,
+        in_specs=[pl.BlockSpec(memory_space=pltpu.VMEM)],
         out_specs=[pl.BlockSpec(memory_space=pl.ANY)] * 4,
         out_shape=[jax.ShapeDtypeStruct(shape, BF16)] * 4,
-        scratch_shapes=[pltpu.VMEM((4, *shape), BF16), sems, sems],
+        scratch_shapes=[pltpu.SemaphoreType.DMA(back.shape[:2])],
+        compiler_params=pltpu.CompilerParams(vmem_limit_bytes=2 * 1024 * 1024),
         name="copy_out",
-    )(*arrays)
+    )(back)
 
 
 def fused_kernel(*refs):
-    xs, flat, outs = refs[0:4], refs[4:8], refs[8:12]
-    (xin, own, far, low, back, orow, ring, row_sum, st_row, st_own, st_far,
+    xs, flat, back = refs[0:4], refs[4:8], refs[8]
+    (xin, own, far, low, orow, ring, row_sum, st_row, st_own, st_far,
      lse_own, lse_far, lse_back, in_sem, a_loc, a_send, a_recv, b_send, bkv_recv,
      bqg_recv, k1_send, k1_recv, k0_send, k0_recv, d2_send, d2_recv, d1_send,
      d1_recv, f1_send, f1_recv, e_send, e_recv, g_send, g_recv, s_send, s_recv, sf_send, sf_recv, l1_send, l1_recv,
-     le_send, le_recv, out_sem) = refs[12:]
+     le_send, le_recv) = refs[9:]
     heads, _, rows = xin.shape[:3]
     chunks = own.shape[0]
     plane_rows, per = own.shape[2], own.shape[3]
@@ -747,11 +739,6 @@
         drain(back.at[h, early, :, ready], e_recv.at[h])
         drain(lse_back.at[h, pl.ds(0, m - 1)], le_recv.at[h])
 
-    def give_out(h, kind):
-        pltpu.make_async_copy(
-            back.at[h, kind], outs[kind].at[:, :, :, lanes_of(h)], out_sem
-        ).start()
-
     def backward_done(h):
         drain(back.at[h, late, :, ready], g_recv.at[h])
 
@@ -763,8 +750,6 @@
             return carry
 
         lax.fori_loop(0, rows, body, 0)
-        give_out(h, 2)
-        give_out(h, 3)
 
     lag_upper, lag_low1, lag_low2, lag_edge1, lag_edge2, lag_rows = LAGS
     pace = splits // rows
@@ -804,11 +789,6 @@
 
             start = jnp.where(last, 0, t % splits // pace)
             lax.fori_loop(start, jnp.where(last, rows, start + 1), body, 0)
-
-        @pl.when((t >= 0) & ((t % splits == splits - 1) & ~last | (t == chunks - splits)))
-        def _():
-            give_out(h, 0)
-            give_out(h, 1)
 
         @pl.when((t >= 0) & (t % splits == splits - 1) & ~last)
         def _():
@@ -890,8 +870,6 @@
     @pl.when(z == 2)
     def _():
         drain(low, d2_send)
-
-    drain(back, out_sem)
 
 
 AHEAD = 2
@@ -929,15 +907,14 @@
     stat = pltpu.VMEM((2 * heads, m, rows, LANES), F32)
     lse = pltpu.VMEM((heads, m, rows, LANES), F32)
     each, by_head, single = dma((chunks,)), dma((heads,)), dma(())
-    outs = pl.pallas_call(
+    back = pl.pallas_call(
         fused_kernel,
         in_specs=[pl.BlockSpec(memory_space=pl.ANY)] * 8,
-        out_specs=[pl.BlockSpec(memory_space=pl.ANY)] * 4,
-        out_shape=[jax.ShapeDtypeStruct(views[0].shape, BF16)] * 4,
+        out_specs=pl.BlockSpec(memory_space=pltpu.VMEM),
+        out_shape=pltpu.VMEM((heads, 4, rows, blocks, GROUP, HEAD_DIM), BF16),
         scratch_shapes=[
             pltpu.VMEM((heads, 4, rows, ROW_LEN, HEAD_DIM), BF16),
             buffer, buffer, buffer,
-            pltpu.VMEM((heads, 4, rows, blocks, GROUP, HEAD_DIM), BF16),
             pltpu.VMEM((heads, rows, HEAD_DIM, ROW_LEN), F32),
             pltpu.VMEM((RING, per, 2, 2 * LANES, HEAD_DIM), F32),
             pltpu.VMEM((rows, 2, ROW_LEN, HEAD_DIM), F32),
@@ -946,10 +923,9 @@
             each, each, each, each, single, each, single,
             each, single, each, single, by_head, single, by_head,
             single, by_head, single, by_head, single, by_head, single, by_head,
-            single,
         ],
         compiler_params=pltpu.CompilerParams(
-            collective_id=0, has_side_effects=True, vmem_limit_bytes=63 * 1024 * 1024
+            collective_id=0, has_side_effects=True, vmem_limit_bytes=50 * 1024 * 1024
         ),
         cost_estimate=pl.CostEstimate(
             flops=tokens * width * 512 * 24,
@@ -958,7 +934,7 @@
         ),
         name="by_planes",
     )(*views, *flat)
-    outs = copy_out(outs)
+    outs = copy_out(back, views[0].shape)
     return tuple(a.reshape(queries.shape) for a in outs)
 
 

time: 227 us -> 223 us (0.982)
  Pallas kernels: 226 us -> 222 us
    pallas_call x1, Pallas kernels: 6.57 us -> 3.42 us  [copy_out(): pl.pallas_call(copy_kernel, in_specs=[pl.BlockSpec(memory_space=pltpu.VME...]
where the time goes in v6:
time: 223 us
  Pallas kernels  222 us (100%)
    pallas_call x1, Pallas kernels, by_planes(): pl.pallas_call(fused_kernel, in_specs=[pl.BlockSpec(memory_space=pl.ANY)]...  218 us

profile of v6, /device:TPU:0, one launch (start us, length us, event | category | flops | bytes accessed | tf_op | source)
XLA Modules:
  0.0 222.5 jit_solution(7020631815955938600)
XLA Ops:
  0.6 218.5 %by_planes.1.refs_0_ = bf16[4,4,4,64,8,128]{5,4,3,2,1,0:T(8,128)(2,1)S(1)} custom-call(bf16[4,64,8,512]{3,2,1,0:T(8,128)(2,1)} %bitcast.12, bf16[4,64,8,512]{3,2,1,0:T(8,128)(2,1)} %bitcast.14, bf16[4,64,8,512]{3,2,1,0:T(8,128)(2,1)} %bitcast.16, bf16[4,64,8,512]{3,2,1,0:T(8,128)(2,1)} %bitcast.18, bf16[4,512,512]{2,1,0:T(8,128)(2,1)} %bitcast.13, ...), custom_call_target="tpu_custom_call" | custom-call | flops 12884901888 | bytes 16777216 | tf_op jit(solution)/shard_map/by_planes/pallas_call | solution.py:910
  219.1 3.4 %copy_out.1 = (bf16[4,64,8,512]{3,2,1,0:T(8,128)(2,1)}, bf16[4,64,8,512]{3,2,1,0:T(8,128)(2,1)}, bf16[4,64,8,512]{3,2,1,0:T(8,128)(2,1)}, bf16[4,64,8,512]{3,2,1,0:T(8,128)(2,1)}) custom-call(bf16[4,4,4,64,8,128]{5,4,3,2,1,0:T(8,128)(2,1)S(1)} %by_planes.1.refs_0_), custom_call_target="tpu_custom_call" | custom-call | tf_op jit(solution)/shard_map/copy_out/pallas_call | solution.py:435

commit v7 on v6

--- a/solution.py
+++ b/solution.py
@@ -811,7 +811,15 @@
         def _():
             pass_far(s - 1)
 
-        @pl.when((s == 0) & outer)
+        @pl.when(s < rows - rows // 2)
+        def _():
+            forward_row(0, rows // 2 + s)
+
+        @pl.when(s == rows - rows // 2 - 1)
+        def _():
+            send_stats(0)
+
+        @pl.when((s == rows - rows // 2 - 1) & outer)
         def _():
             pass_stats(0)
 
@@ -845,8 +853,7 @@
         forward_row(0, r)
         return carry
 
-    lax.fori_loop(0, rows, first_head, 0)
-    send_stats(0)
+    lax.fori_loop(0, rows // 2, first_head, 0)
     lax.fori_loop(0, chunks + max(LAGS), step, 0)
     backward_done(heads - 1)
 

time: 223 us -> 222 us (level)
  no operation moved by 1% of the time
where the time goes in v7:
time: 222 us
  Pallas kernels  221 us (100%)
    pallas_call x1, Pallas kernels, by_planes(): pl.pallas_call(fused_kernel, in_specs=[pl.BlockSpec(memory_space=pl.ANY)]...  218 us

profile of v7, /device:TPU:0, one launch (start us, length us, event | category | flops | bytes accessed | tf_op | source)
XLA Modules:
  0.0 221.9 jit_solution(17993318784635827772)
XLA Ops:
  0.6 217.8 %by_planes.1.refs_0_ = bf16[4,4,4,64,8,128]{5,4,3,2,1,0:T(8,128)(2,1)S(1)} custom-call(bf16[4,64,8,512]{3,2,1,0:T(8,128)(2,1)} %bitcast.12, bf16[4,64,8,512]{3,2,1,0:T(8,128)(2,1)} %bitcast.14, bf16[4,64,8,512]{3,2,1,0:T(8,128)(2,1)} %bitcast.16, bf16[4,64,8,512]{3,2,1,0:T(8,128)(2,1)} %bitcast.18, bf16[4,512,512]{2,1,0:T(8,128)(2,1)} %bitcast.13, ...), custom_call_target="tpu_custom_call" | custom-call | flops 12884901888 | bytes 16777216 | tf_op jit(solution)/shard_map/by_planes/pallas_call | solution.py:917
  218.5 3.4 %copy_out.1 = (bf16[4,64,8,512]{3,2,1,0:T(8,128)(2,1)}, bf16[4,64,8,512]{3,2,1,0:T(8,128)(2,1)}, bf16[4,64,8,512]{3,2,1,0:T(8,128)(2,1)}, bf16[4,64,8,512]{3,2,1,0:T(8,128)(2,1)}) custom-call(bf16[4,4,4,64,8,128]{5,4,3,2,1,0:T(8,128)(2,1)S(1)} %by_planes.1.refs_0_), custom_call_target="tpu_custom_call" | custom-call | tf_op jit(solution)/shard_map/copy_out/pallas_call | solution.py:435
